TPU v7x, 32 devices: a 4x2x2 block of a 4x4x8 slice. The times are simulated.
32 devices in a mesh: dp: 4 (over y, z), tp: 8 (over x, core).
Axes of the slice: x: 4, y: 2, z: 2, core: 2. Of those that a mesh axis runs over, the one named last changes fastest.
The devices are a block of a 4x4x8 slice.
Arguments:
- x_seq: bfloat16 [24, 2048, 2048], P('dp', 'tp'), parts along dimension 0
- ln_gain: float32 [2048], replicated
- ln_bias: float32 [2048], replicated
- w_qkv: bfloat16 [2048, 8, 3, 256], P(None, 'tp')
- w_out: bfloat16 [2048, 2048], P('tp')
- w_up: bfloat16 [2048, 8192], P(None, 'tp')
- w_down: bfloat16 [8192, 2048], P('tp')
Outputs:
- output: bfloat16 [24, 2048, 2048], P('dp', 'tp'), parts along dimension 0
There are 4 independent parts. A program takes and returns all parts, laid end to end along the dimension named above; an argument that names none is the same for every part.
All inputs are finite; a program needn't handle non-finite values.
Results may differ from a plain program's by a relative error of at most 0.0116155.
Values are sent between devices in bfloat16 or wider.
A program may use at most 768 MiB of HBM per device.

v0:
```python
import jax
import jax.numpy as jnp
from jax import lax
from jax.sharding import PartitionSpec as P, NamedSharding

LN_EPS = 1e-5


def layer_norm(x_f32, ln_gain, ln_bias):
    row_mean = jnp.mean(x_f32, axis=-1, keepdims=True)
    centered = x_f32 - row_mean
    variance = jnp.mean(centered * centered, axis=-1, keepdims=True)
    return centered * lax.rsqrt(variance + LN_EPS) * ln_gain + ln_bias


def solution(mesh):
    def local_layer(x_blk, ln_gain, ln_bias, w_qkv, w_out, w_up, w_down):
        x_full = lax.all_gather(x_blk, "tp", axis=1, tiled=True)
        seq_len = x_full.shape[1]
        model_dim = x_full.shape[2]
        kv_local, group_width, head_dim = w_qkv.shape[1:]
        group_q = group_width - 2
        normed = layer_norm(x_full.astype(jnp.float32), ln_gain, ln_bias).astype(jnp.bfloat16)
        proj_qkv = jnp.einsum("bsd,dgjh->bsgjh", normed, w_qkv,
                              preferred_element_type=jnp.float32).astype(jnp.bfloat16)
        queries = proj_qkv[:, :, :, :group_q]
        key_rows = proj_qkv[:, :, :, group_q]
        value_rows = proj_qkv[:, :, :, group_q + 1]
        scores = jnp.einsum("bsgjh,btgh->bgjst", queries, key_rows,
                            preferred_element_type=jnp.float32) * (head_dim ** -0.5)
        causal = (lax.broadcasted_iota(jnp.int32, (seq_len, seq_len), 0)
                  >= lax.broadcasted_iota(jnp.int32, (seq_len, seq_len), 1))
        scores = jnp.where(causal, scores, -jnp.inf)
        attn_prob = jax.nn.softmax(scores, axis=-1).astype(jnp.bfloat16)
        context = jnp.einsum("bgjst,btgh->bgjsh", attn_prob, value_rows,
                             preferred_element_type=jnp.float32).astype(jnp.bfloat16)
        w_heads = w_out.reshape(kv_local, group_q, head_dim, model_dim)
        attn_part = jnp.einsum("bgjsh,gjhd->bsd", context, w_heads, preferred_element_type=jnp.float32)
        hidden = jnp.einsum("bsd,df->bsf", normed, w_up, preferred_element_type=jnp.float32)
        activated = jax.nn.gelu(hidden, approximate=False).astype(jnp.bfloat16)
        mlp_part = jnp.einsum("bsf,fd->bsd", activated, w_down, preferred_element_type=jnp.float32)
        branch_part = (attn_part + mlp_part).astype(jnp.bfloat16)
        branch = lax.psum_scatter(branch_part, "tp", scatter_dimension=1, tiled=True)
        return (x_blk.astype(jnp.float32) + branch.astype(jnp.float32)).astype(jnp.bfloat16)

    return jax.shard_map(
        local_layer, mesh=mesh,
        in_specs=(P("dp", "tp", None), P(), P(), P(None, "tp", None, None),
                  P("tp", None), P(None, "tp"), P("tp", None)),
        out_specs=P("dp", "tp", None), check_vma=False)
```

profile of v0, /device:TPU:81, one launch (start us, length us, event | category | flops | bytes accessed | tf_op | source)
XLA Modules:
  0.0 989.3 jit_solution(8769174729803832254)
XLA Ops:
  6.5 0.0 copy-start
  6.6 0.0 all-gather.2.cloned.1.call-start
  6.6 0.7 all-gather.2.cloned.1.call-update
  7.3 0.1 reduce-scatter.2.cloned.1.call-start
  7.4 4.1 iota_compare_fusion
  11.5 0.0 copy-start.7
  11.5 0.0 copy-start.9
  11.5 227.0 %all-gather.2.cloned.1.call-done = bf16[6,2048,2048]{2,1,0:T(8,128)(2,1)} async-done(((bf16[6,256,2048]{2,1,0:T(8,128)(2,1)}), bf16[6,2048,2048]{2,1,0:T(8,128)(2,1)}) %all-gather.2.cloned.1.call-update) | async-done | bytes 50331664 | tf_op jit(solution)/shard_map/all_gather | solution.py:18
  238.4 16.0 %convert_reduce_fusion = f32[6,2048]{1,0:T(8,128)S(1)} fusion(bf16[6,2048,2048]{2,1,0:T(8,128)(2,1)} %all-gather.2.cloned.1.call-done), kind=kLoop, calls=%fused_computation.1 | loop fusion | flops 50319360 | bytes 50380800 | tf_op jit(solution)/shard_map/reduce_sum | solution.py:10
  254.4 0.0 copy-start.3
  254.4 18.4 %fusion.2 = f32[6,2048]{1,0:T(8,128)S(1)} fusion(bf16[6,2048,2048]{2,1,0:T(8,128)(2,1)} %all-gather.2.cloned.1.call-done, f32[6,2048]{1,0:T(8,128)S(1)} %broadcast_multiply_fusion), kind=kLoop, calls=%fused_computation.4 | loop fusion | flops 100651008 | bytes 50429952 | tf_op jit(solution)/shard_map/reduce_sum | solution.py:12
  272.8 0.0 copy-done
  272.8 0.0 copy-done.7
  272.9 0.0 copy-done.9
  272.9 0.0 copy-start.5
  272.9 54.9 %convert_bitcast_fusion = bf16[6,2048,1,3,256]{4,1,3,0,2:T(8,128)(2,1)} fusion(f32[2048]{0:T(1024)S(1)} %copy-done.7, f32[2048]{0:T(1024)S(1)} %copy-done.9, f32[6,2048]{1,0:T(8,128)S(1)} %add_rsqrt_fusion, f32[6,2048]{1,0:T(8,128)S(1)} %broadcast_multiply_fusion, bf16[6,2048,2048]{2,1,0:T(8,128)(2,1)} %all-gather.2.cloned.1.call-done, ...), kind=kOutput, calls=%fused_computation.72 | convolution fusion | flops 38815137792 | bytes 72466432 | tf_op jit(solution)/shard_map/bsd,dgjh->bsgjh/dot_general | solution.py:24
  327.8 0.0 copy-done.3
  327.8 0.0 copy-done.5
  327.8 39.8 %fusion.7 = (f32[6,2048]{1,0:T(8,128)S(1)}, f32[6,2048,2048]{2,1,0:T(8,128)}) fusion(pred[2048,2048]{0,1:T(8,128)(4,1)} %iota_compare_fusion, bf16[6,2048,1,3,256]{4,1,3,0,2:T(8,128)(2,1)} %convert_bitcast_fusion), kind=kOutput, calls=%fused_computation.13 | convolution fusion | flops 12960387072 | bytes 117489664 | tf_op jit(solution)/shard_map/bsgjh,btgh->bgjst/dot_general | solution.py:29
  367.5 35.2 %fusion.6 = f32[6,2048]{1,0:T(8,128)S(1)} fusion(f32[6,2048,2048]{2,1,0:T(8,128)} %get-tuple-element.8, f32[6,2048]{1,0:T(8,128)S(1)} %get-tuple-element.7, pred[2048,2048]{0,1:T(8,128)(4,1)} %iota_compare_fusion), kind=kLoop, calls=%fused_computation.12 | loop fusion | flops 100651008 | bytes 104955904 | tf_op jit(solution)/shard_map/reduce_sum | solution.py:34
  402.7 0.0 copy-start.2
  402.7 43.5 %fusion.120 = bf16[6,2048,256]{2,1,0:T(8,128)(2,1)} fusion(bf16[6,2048,1,3,256]{4,1,3,0,2:T(8,128)(2,1)} %convert_bitcast_fusion, f32[6,2048]{1,0:T(8,128)S(1)} %fusion.6, f32[6,2048]{1,0:T(8,128)S(1)} %get-tuple-element.7, f32[6,2048,2048]{2,1,0:T(8,128)} %get-tuple-element.8, pred[2048,2048]{0,1:T(8,128)(4,1)} %iota_compare_fusion), kind=kOutput, calls=%fused_computation.84.clone.1 | convolution fusion | flops 13013876736 | bytes 117538816 | tf_op jit(solution)/shard_map/bgjst,btgh->bgjsh/dot_general | solution.py:35
  446.2 0.0 copy-done.2
  446.2 0.0 copy-start.4
  446.2 0.0 copy-start.6
  446.2 0.0 copy-start.8
  446.2 0.0 copy-start.10
  446.2 37.5 %fusion.63 = f32[6,2048,2048]{2,1,0:T(8,128)} fusion(bf16[256,2048]{1,0:T(8,128)(2,1)S(1)} %copy-done.2, bf16[6,2048,256]{2,1,0:T(8,128)(2,1)} %fusion.120), kind=kOutput, calls=%fused_computation.83 | convolution fusion | flops 12884901888 | bytes 108003328 | tf_op jit(solution)/shard_map/bgjsh,gjhd->bsd/dot_general | solution.py:38
  483.7 0.0 copy-done.4
  483.7 0.0 copy-done.6
  483.7 0.0 copy-done.8
  483.7 0.0 copy-done.10
  483.7 76.6 %fusion.59 = (u8[2048,1024]{1,0:T(8,128)(4,1)}, u8[2048,1024]{1,0:T(8,128)(4,1)}, f32[6,2048,1024]{2,1,0:T(8,128)}) fusion(bf16[2048,1024]{1,0:T(8,128)(2,1)} %param.12, bf16[6,2048,2048]{2,1,0:T(8,128)(2,1)} %all-gather.2.cloned.1.call-done, f32[2048]{0:T(1024)S(1)} %copy-done.8, f32[2048]{0:T(1024)S(1)} %copy-done.10, f32[6,2048]{1,0:T(8,128)S(1)} %copy-done.6, ...), kind=kOutput, calls=%fused_computation.76 | convolution fusion | flops 51849986048 | bytes 109166592 | tf_op jit(solution)/shard_map/bsd,df->bsf/dot_general | solution.py:39
  560.4 0.0 copy-start.1
  560.4 165.2 %add_convert_fusion = bf16[6,2048,2048]{2,1,0:T(8,128)(2,1)} fusion(f32[6,2048,2048]{2,1,0:T(8,128)} %fusion.63, f32[6,2048,1024]{2,1,0:T(8,128)} %get-tuple-element.9, u8[2048,1024]{1,0:T(8,128)(4,1)} %get-tuple-element.6, u8[2048,1024]{1,0:T(8,128)(4,1)} %get-tuple-element.5, bf16[1024,2048]{1,0:T(8,128)(2,1)} %param.13), kind=kOutput, calls=%fused_computation.9 | convolution fusion | flops 52470743040 | bytes 209715200 | tf_op jit(solution)/shard_map/bsf,fd->bsd/dot_general | solution.py:41
  725.6 0.1 reduce-scatter.2.cloned.1.call-update
  725.7 245.3 %reduce-scatter.2.cloned.1.call-done = bf16[6,256,2048]{2,1,0:T(8,128)(2,1)} async-done(((bf16[6,2048,2048]{2,1,0:T(8,128)(2,1)}), bf16[6,256,2048]{2,1,0:T(8,128)(2,1)}) %reduce-scatter.2.cloned.1.call-update) | async-done | bytes 6291472 | tf_op jit(solution)/shard_map/reduce_scatter | solution.py:43
  970.9 11.0 %add_convert_fusion.1 = bf16[6,256,2048]{2,1,0:T(8,128)(2,1)} fusion(bf16[6,256,2048]{2,1,0:T(8,128)(2,1)} %reduce-scatter.2.cloned.1.call-done, bf16[6,256,2048]{2,1,0:T(8,128)(2,1)} %param.7), kind=kLoop, calls=%fused_computation.74 | loop fusion | flops 12582912 | bytes 18874368 | tf_op jit(solution)/shard_map/convert_element_type | solution.py:44
  981.9 0.0 copy-done.1
  (2 shorter events, 0.0 us)
Async XLA Ops:
  6.5 266.3 %copy-start = (bf16[2048,1,3,256]{3,0,2,1:T(8,128)(2,1)S(1)}, bf16[2048,1,3,256]{3,0,2,1:T(8,128)(2,1)}, u32[]{:S(2)}) copy-start(bf16[2048,1,3,256]{3,0,2,1:T(8,128)(2,1)} %param.10) | copy-start | bytes 9437188
  6.6 231.9 %all-gather.2.cloned.1.call-start = ((), (), s32[]{:S(2)}) async-start(), calls=%async_computation.1 | async-start | bytes 56623104 | tf_op jit(solution)/shard_map/all_gather | solution.py:18
  7.3 963.6 %reduce-scatter.2.cloned.1.call-start = ((), (), s32[]{:S(2)}) async-start(), calls=%async_computation.2 | async-start | bytes 56623104 | tf_op jit(solution)/shard_map/reduce_scatter | solution.py:43
  11.5 261.4 %copy-start.7 = (f32[2048]{0:T(1024)S(1)}, f32[2048]{0:T(1024)}, u32[]{:S(2)}) copy-start(f32[2048]{0:T(1024)} %param.9) | copy-start | bytes 24580
  11.5 261.4 %copy-start.9 = (f32[2048]{0:T(1024)S(1)}, f32[2048]{0:T(1024)}, u32[]{:S(2)}) copy-start(f32[2048]{0:T(1024)} %param.8) | copy-start | bytes 24580
  254.4 73.3 %copy-start.3 = (f32[6,2048]{1,0:T(8,128)}, f32[6,2048]{1,0:T(8,128)S(1)}, u32[]{:S(2)}) copy-start(f32[6,2048]{1,0:T(8,128)S(1)} %broadcast_multiply_fusion) | copy-start | bytes 147460
  272.9 54.9 %copy-start.5 = (f32[6,2048]{1,0:T(8,128)}, f32[6,2048]{1,0:T(8,128)S(1)}, u32[]{:S(2)}) copy-start(f32[6,2048]{1,0:T(8,128)S(1)} %add_rsqrt_fusion) | copy-start | bytes 147460
  402.7 43.5 %copy-start.2 = (bf16[256,2048]{1,0:T(8,128)(2,1)S(1)}, bf16[256,2048]{1,0:T(8,128)(2,1)}, u32[]{:S(2)}) copy-start(bf16[256,2048]{1,0:T(8,128)(2,1)} %param.11) | copy-start | bytes 3145732
  446.2 37.5 %copy-start.4 = (f32[6,2048]{1,0:T(8,128)S(1)}, f32[6,2048]{1,0:T(8,128)}, u32[]{:S(2)}) copy-start(f32[6,2048]{1,0:T(8,128)} %copy-done.3) | copy-start | bytes 147460
  446.2 37.5 %copy-start.6 = (f32[6,2048]{1,0:T(8,128)S(1)}, f32[6,2048]{1,0:T(8,128)}, u32[]{:S(2)}) copy-start(f32[6,2048]{1,0:T(8,128)} %copy-done.5) | copy-start | bytes 147460
  446.2 37.5 %copy-start.8 = (f32[2048]{0:T(1024)S(1)}, f32[2048]{0:T(1024)}, u32[]{:S(2)}) copy-start(f32[2048]{0:T(1024)} %param.9) | copy-start | bytes 24580
  446.2 37.5 %copy-start.10 = (f32[2048]{0:T(1024)S(1)}, f32[2048]{0:T(1024)}, u32[]{:S(2)}) copy-start(f32[2048]{0:T(1024)} %param.8) | copy-start | bytes 24580
  560.4 421.6 %copy-start.1 = (bf16[2048,1,3,256]{3,0,2,1:T(8,128)(2,1)S(1)}, bf16[2048,1,3,256]{3,0,2,1:T(8,128)(2,1)}, u32[]{:S(2)}) copy-start(bf16[2048,1,3,256]{3,0,2,1:T(8,128)(2,1)} %param.10) | copy-start | bytes 9437188
Sparse Core Ops, SparseCore 0:
  9.0 229.4 all-gather.1
  725.8 245.0 reduce-scatter.1
where the time goes:
time: 998 us; the launch traced here: 989 us
  waiting for transfers between devices  473 us (47%)
  matrix products  417 us (42%)
  other arithmetic  84.6 us (8%)
  between operations  14.1 us (1%)
    reduce_scatter x1, waiting for transfers between devices, local_layer(): lax.psum_scatter(branch_part, 'tp', scatter_dimension=1, tiled=True)  245 us
    all_gather x1, waiting for transfers between devices, local_layer(): x_full = lax.all_gather(x_blk, 'tp', axis=1, tiled=True)  227 us
    dot_general x1, matrix products, local_layer(): jnp.einsum('bsf,fd->bsd', activated, w_down, preferred_element_type=jnp.f...  165 us
    dot_general x1, matrix products, local_layer(): jnp.einsum('bsd,df->bsf', normed, w_up, preferred_element_type=jnp.float32)  76.6 us
    dot_general x1, matrix products, local_layer(): jnp.einsum('bsd,dgjh->bsgjh', normed, w_qkv, preferred_element_type=jnp.f...  54.9 us
    dot_general x1, matrix products, local_layer(): jnp.einsum('bgjst,btgh->bgjsh', attn_prob, value_rows, preferred_element_...  43.5 us
    dot_general x1, matrix products, local_layer(): jnp.einsum('bsgjh,btgh->bgjst', queries, key_rows, preferred_element_type...  39.8 us
    dot_general x1, matrix products, local_layer(): jnp.einsum('bgjsh,gjhd->bsd', context, w_heads, preferred_element_type=jn...  37.5 us
  transfers between devices with their start and end apart: 2, of which 2 were waited for; matrix products, arithmetic and copies ran while one was open for 0% of the time, Pallas kernels for 0%

commit v1 on v0

v1 whole, which is shorter than its diff:
```python
import jax
import jax.numpy as jnp
from jax import lax
from jax.sharding import PartitionSpec as P

LN_EPS = 1e-5


def layer_norm(x_f32, ln_gain, ln_bias):
    row_mean = jnp.mean(x_f32, axis=-1, keepdims=True)
    centered = x_f32 - row_mean
    variance = jnp.mean(centered * centered, axis=-1, keepdims=True)
    return centered * lax.rsqrt(variance + LN_EPS) * ln_gain + ln_bias


def solution(mesh):
    def local_layer(x_blk, ln_gain, ln_bias, w_qkv, w_out, w_up, w_down):
        kv_local, group_width, head_dim = w_qkv.shape[1:]
        group_q = group_width - 2
        w_heads = w_out.reshape(kv_local, group_q, head_dim, w_out.shape[-1])

        def one_sequence(x_seq):
            x_full = lax.all_gather(x_seq, "tp", axis=0, tiled=True)
            seq_len = x_full.shape[0]
            normed = layer_norm(x_full.astype(jnp.float32), ln_gain, ln_bias).astype(jnp.bfloat16)
            proj_qkv = jnp.einsum("sd,dgjh->gjsh", normed, w_qkv,
                                  preferred_element_type=jnp.float32).astype(jnp.bfloat16)
            queries = proj_qkv[:, :group_q]
            key_rows = proj_qkv[:, group_q]
            value_rows = proj_qkv[:, group_q + 1]
            scores = jnp.einsum("gjsh,gth->gjst", queries, key_rows,
                                preferred_element_type=jnp.float32) * (head_dim ** -0.5)
            causal = (lax.broadcasted_iota(jnp.int32, (seq_len, seq_len), 0)
                      >= lax.broadcasted_iota(jnp.int32, (seq_len, seq_len), 1))
            scores = jnp.where(causal, scores, -jnp.inf)
            attn_prob = jax.nn.softmax(scores, axis=-1).astype(jnp.bfloat16)
            context = jnp.einsum("gjst,gth->gjsh", attn_prob, value_rows,
                                 preferred_element_type=jnp.float32).astype(jnp.bfloat16)
            attn_part = jnp.einsum("gjsh,gjhd->sd", context, w_heads, preferred_element_type=jnp.float32)
            hidden = jnp.einsum("sd,df->sf", normed, w_up, preferred_element_type=jnp.float32)
            activated = jax.nn.gelu(hidden, approximate=False).astype(jnp.bfloat16)
            mlp_part = jnp.einsum("sf,fd->sd", activated, w_down, preferred_element_type=jnp.float32)
            branch_part = (attn_part + mlp_part).astype(jnp.bfloat16)
            branch = lax.psum_scatter(branch_part, "tp", scatter_dimension=0, tiled=True)
            return (x_seq.astype(jnp.float32) + branch.astype(jnp.float32)).astype(jnp.bfloat16)

        return jnp.stack([one_sequence(x_blk[i]) for i in range(x_blk.shape[0])])

    return jax.shard_map(
        local_layer, mesh=mesh,
        in_specs=(P("dp", "tp", None), P(), P(), P(None, "tp", None, None),
                  P("tp", None), P(None, "tp"), P("tp", None)),
        out_specs=P("dp", "tp", None), check_vma=False)
```

time: 998 us -> 909 us (0.911)
  waiting for transfers between devices: 473 us -> 303 us
  local copies, waits for them, and re-layouts: 0.05 us -> 44.7 us
  matrix products: 417 us -> 438 us
    reduce_scatter x1 -> x6, waiting for transfers between devices: 245 us -> 86.1 us  [one_sequence(): lax.psum_scatter(branch_part, 'tp', scatter_dimension=0, tiled=True)]
    unnamed x22 -> x66, local copies, waits for them, and re-layouts: 0.05 us -> 42.2 us
    dot_general x6 -> x24, matrix products: 417 us -> 438 us  [the longest x6 260 us: one_sequence(): jnp.einsum('sf,fd->sd', activated, w_down, preferred_element_type=jnp.flo...]
    all_gather x1 -> x6, waiting for transfers between devices: 227 us -> 214 us  [one_sequence(): x_full = lax.all_gather(x_seq, 'tp', axis=0, tiled=True)]
    reduce_sum x1 -> x6, other arithmetic: 16 us -> 28.3 us  [layer_norm(): row_mean = jnp.mean(x_f32, axis=-1, keepdims=True)]
    unnamed x0 -> x4, other arithmetic: none -> 11.6 us
    convert_element_type x1 -> x0, other arithmetic: 11 us -> none  [local_layer(): (x_blk.astype(jnp.float32) + branch.astype(jnp.float32)).astype(jnp.bfloa...]
    reduce_sum x1 -> x6, other arithmetic: 35.2 us -> 27.9 us  [one_sequence(): attn_prob = jax.nn.softmax(scores, axis=-1).astype(jnp.bfloat16)]
  transfers between devices with their start and end apart: 2 -> 12, of which waited for: 2 -> 7; matrix products, arithmetic and copies ran while one was open for 0% -> 49% of each run, Pallas kernels for 0% -> 0%
where the time goes in v1:
time: 909 us; the launch traced here: 895 us
  matrix products  438 us (48%)
  waiting for transfers between devices  303 us (33%)
  other arithmetic  93.5 us (10%)
  local copies, waits for them, and re-layouts  44.7 us (5%)
  between operations  14.5 us (2%)
    dot_general x6, matrix products, one_sequence(): jnp.einsum('sf,fd->sd', activated, w_down, preferred_element_type=jnp.flo...  260 us
    all_gather x6, waiting for transfers between devices, one_sequence(): x_full = lax.all_gather(x_seq, 'tp', axis=0, tiled=True)  214 us
    dot_general x6, matrix products, one_sequence(): jnp.einsum('gjsh,gjhd->sd', context, w_heads, preferred_element_type=jnp....  106 us
    reduce_scatter x6, waiting for transfers between devices, one_sequence(): lax.psum_scatter(branch_part, 'tp', scatter_dimension=0, tiled=True)  86.1 us
    dot_general x6, matrix products, one_sequence(): jnp.einsum('sd,dgjh->gjsh', normed, w_qkv, preferred_element_type=jnp.flo...  58 us
    unnamed x66, local copies, waits for them, and re-layouts  42.2 us
    reduce_sum x6, other arithmetic, layer_norm(): row_mean = jnp.mean(x_f32, axis=-1, keepdims=True)  28.3 us
    reduce_sum x6, other arithmetic, one_sequence(): attn_prob = jax.nn.softmax(scores, axis=-1).astype(jnp.bfloat16)  27.9 us
  transfers between devices with their start and end apart: 12, of which 7 were waited for; matrix products, arithmetic and copies ran while one was open for 49% of the time, Pallas kernels for 0%

profile of v1, /device:TPU:81, one launch (start us, length us, event | category | flops | bytes accessed | tf_op | source)
XLA Modules:
  0.0 894.8 jit_solution(10677236543113477445)
XLA Ops:
  6.6 2.5 slice.72
  9.2 51.0 %all-gather.13.cloned.1.call-done = bf16[1,2048,2048]{2,1,0:T(8,128)(2,1)} async-done(((bf16[1,256,2048]{2,1,0:T(8,128)(2,1)}), bf16[1,2048,2048]{2,1,0:T(8,128)(2,1)}) %all-gather.13.cloned.1.call-update) | async-done | bytes 8388624 | tf_op jit(solution)/shard_map/all_gather | solution.py:23
  60.2 4.7 convert_reduce_fusion.5
  66.0 2.3 fusion.3
  68.3 7.9 fusion.373
  76.3 2.4 fusion.48
  78.7 5.7 copy-done.7
  84.4 4.7 fusion.42
  89.1 43.3 %fusion.142 = f32[2048,2048]{1,0:T(8,128)} fusion(bf16[1024,2048]{1,0:T(8,128)(2,1)} %param.13, bf16[2048,1024]{1,0:T(8,128)(2,1)} %param.12, bf16[1,2048,2048]{2,1,0:T(8,128)(2,1)} %all-gather.13.cloned.1.call-done, f32[2048]{0:T(1024)S(1)} %copy-done.25, f32[2048]{0:T(1024)S(1)} %copy-done.26, f32[2048]{0:T(1024)S(1)} %add_rsqrt_fusion.5, ...), kind=kOutput, calls=%fused_computation.228 | convolution fusion | flops 17341349888 | bytes 33587200 | tf_op jit(solution)/shard_map/sf,fd->sd/dot_general | solution.py:42
  132.4 17.7 %add_convert_fusion.5 = bf16[2048,2048]{1,0:T(8,128)(2,1)} fusion(f32[2048,2048]{1,0:T(8,128)} %fusion.142, bf16[256,2048]{1,0:T(8,128)(2,1)} %param.11, f32[2048,2048]{0,1:T(8,128)} %copy-done.7, f32[2048]{0:T(1024)S(1)} %fusion.42, f32[2048]{0:T(1024)S(1)} %get-tuple-element.11, bf16[1,3,2048,256]{3,2,1,0:T(8,128)(2,1)} %copy-done.27), kind=kOutput, calls=%fused_computation.74 | convolution fusion | flops 4329046016 | bytes 44056576 | tf_op jit(solution)/shard_map/gjsh,gjhd->sd/dot_general | solution.py:39
  150.2 48.8 %reduce-scatter.7.cloned.1.call-done = bf16[256,2048]{1,0:T(8,128)(2,1)} async-done(((bf16[2048,2048]{1,0:T(8,128)(2,1)}), bf16[256,2048]{1,0:T(8,128)(2,1)}) %reduce-scatter.7.cloned.1.call-update) | async-done | bytes 1048592 | tf_op jit(solution)/shard_map/reduce_scatter | solution.py:44
  199.0 6.3 fusion.654
  208.3 44.3 %all-gather.15.cloned.1.call-done = bf16[1,2048,2048]{2,1,0:T(8,128)(2,1)} async-done(((bf16[1,256,2048]{2,1,0:T(8,128)(2,1)}), bf16[1,2048,2048]{2,1,0:T(8,128)(2,1)}) %all-gather.15.cloned.1.call-update) | async-done | bytes 8388624 | tf_op jit(solution)/shard_map/all_gather | solution.py:23
  252.5 4.7 convert_reduce_fusion.4
  258.3 2.3 fusion.10
  260.6 40.0 %all-gather.17.cloned.1.call-done = bf16[1,2048,2048]{2,1,0:T(8,128)(2,1)} async-done(((bf16[1,256,2048]{2,1,0:T(8,128)(2,1)}), bf16[1,2048,2048]{2,1,0:T(8,128)(2,1)}) %all-gather.17.cloned.1.call-update) | async-done | bytes 8388624 | tf_op jit(solution)/shard_map/all_gather | solution.py:23
  300.7 4.7 convert_reduce_fusion.3
  305.4 1.1 copy-done.4
  306.5 2.3 fusion.17
  309.4 39.4 %all-gather.19.cloned.1.call-done = bf16[1,2048,2048]{2,1,0:T(8,128)(2,1)} async-done(((bf16[1,256,2048]{2,1,0:T(8,128)(2,1)}), bf16[1,2048,2048]{2,1,0:T(8,128)(2,1)}) %all-gather.19.cloned.1.call-update) | async-done | bytes 8388624 | tf_op jit(solution)/shard_map/all_gather | solution.py:23
  348.8 4.7 convert_reduce_fusion.2
  353.5 1.1 copy-done.3
  354.6 2.3 fusion.24
  357.5 39.4 %all-gather.21.cloned.1.call-done = bf16[1,2048,2048]{2,1,0:T(8,128)(2,1)} async-done(((bf16[1,256,2048]{2,1,0:T(8,128)(2,1)}), bf16[1,2048,2048]{2,1,0:T(8,128)(2,1)}) %all-gather.21.cloned.1.call-update) | async-done | bytes 8388624 | tf_op jit(solution)/shard_map/all_gather | solution.py:23
  397.0 4.8 convert_reduce_fusion.1
  402.7 2.3 fusion.31
  405.7 10.0 %fusion.368 = bf16[1,3,2048,256]{3,2,1,0:T(8,128)(2,1)S(1)} fusion(bf16[2048,1,3,256]{3,0,2,1:T(8,128)(2,1)S(1)} %copy-done, bf16[1,2048,2048]{2,1,0:T(8,128)(2,1)} %all-gather.15.cloned.1.call-done, f32[2048]{0:T(1024)S(1)} %add_rsqrt_fusion.4, f32[2048]{0:T(1024)S(1)} %broadcast_multiply_fusion.4, f32[2048]{0:T(1024)S(1)} %copy-done.25, ...), kind=kOutput, calls=%fused_computation.425 | convolution fusion | flops 6469189632 | bytes 14712832 | tf_op jit(solution)/shard_map/sd,dgjh->gjsh/dot_general | solution.py:26
  415.7 2.4 fusion.49
  418.1 5.7 copy-done.8
  423.8 4.7 fusion.43
  428.5 43.3 %fusion.140 = f32[2048,2048]{1,0:T(8,128)} fusion(bf16[1024,2048]{1,0:T(8,128)(2,1)} %param.13, bf16[2048,1024]{1,0:T(8,128)(2,1)} %param.12, bf16[1,2048,2048]{2,1,0:T(8,128)(2,1)} %all-gather.15.cloned.1.call-done, f32[2048]{0:T(1024)S(1)} %add_rsqrt_fusion.4, f32[2048]{0:T(1024)S(1)} %broadcast_multiply_fusion.4, f32[2048]{0:T(1024)S(1)} %copy-done.25, ...), kind=kOutput, calls=%fused_computation.227 | convolution fusion | flops 17341349888 | bytes 33587200 | tf_op jit(solution)/shard_map/sf,fd->sd/dot_general | solution.py:42
  471.8 17.7 %add_convert_fusion.4 = bf16[2048,2048]{1,0:T(8,128)(2,1)} fusion(f32[2048,2048]{1,0:T(8,128)} %fusion.140, bf16[256,2048]{1,0:T(8,128)(2,1)} %param.11, f32[2048,2048]{0,1:T(8,128)} %copy-done.8, f32[2048]{0:T(1024)S(1)} %fusion.43, f32[2048]{0:T(1024)S(1)} %get-tuple-element.13, bf16[1,3,2048,256]{3,2,1,0:T(8,128)(2,1)} %copy-done.28), kind=kOutput, calls=%fused_computation.70 | convolution fusion | flops 4329046016 | bytes 44056576 | tf_op jit(solution)/shard_map/gjsh,gjhd->sd/dot_general | solution.py:39
  489.7 4.7 convert_reduce_fusion
  495.4 2.3 fusion.38
  498.4 10.0 %fusion.363 = bf16[1,3,2048,256]{3,2,1,0:T(8,128)(2,1)S(1)} fusion(bf16[2048,1,3,256]{3,0,2,1:T(8,128)(2,1)S(1)} %copy-done, bf16[1,2048,2048]{2,1,0:T(8,128)(2,1)} %all-gather.17.cloned.1.call-done, f32[2048]{0:T(1024)S(1)} %copy-done.24, f32[2048]{0:T(1024)S(1)} %copy-done.20, f32[2048]{0:T(1024)S(1)} %copy-done.25, f32[2048]{0:T(1024)S(1)} %copy-done.26), kind=kOutput, calls=%fused_computation.424 | convolution fusion | flops 6469189632 | bytes 14712832 | tf_op jit(solution)/shard_map/sd,dgjh->gjsh/dot_general | solution.py:26
  508.4 2.4 fusion.50
  510.8 5.7 copy-done.9
  516.5 4.7 fusion.44
  521.2 43.3 %fusion.138 = f32[2048,2048]{1,0:T(8,128)} fusion(bf16[1024,2048]{1,0:T(8,128)(2,1)} %param.13, bf16[2048,1024]{1,0:T(8,128)(2,1)} %param.12, bf16[1,2048,2048]{2,1,0:T(8,128)(2,1)} %all-gather.17.cloned.1.call-done, f32[2048]{0:T(1024)S(1)} %copy-done.24, f32[2048]{0:T(1024)S(1)} %copy-done.20, f32[2048]{0:T(1024)S(1)} %copy-done.25, f32[2048]{0:T(1024)S(1)} %copy-done.26), kind=kOutput, calls=%fused_computation.226 | convolution fusion | flops 17341349888 | bytes 33587200 | tf_op jit(solution)/shard_map/sf,fd->sd/dot_general | solution.py:42
  564.5 17.7 %add_convert_fusion.3 = bf16[2048,2048]{1,0:T(8,128)(2,1)} fusion(f32[2048,2048]{1,0:T(8,128)} %fusion.138, bf16[256,2048]{1,0:T(8,128)(2,1)} %param.11, f32[2048,2048]{0,1:T(8,128)} %copy-done.9, f32[2048]{0:T(1024)S(1)} %fusion.44, f32[2048]{0:T(1024)S(1)} %get-tuple-element.15, bf16[1,3,2048,256]{3,2,1,0:T(8,128)(2,1)} %copy-done.29), kind=kOutput, calls=%fused_computation.66 | convolution fusion | flops 4329046016 | bytes 44056576 | tf_op jit(solution)/shard_map/gjsh,gjhd->sd/dot_general | solution.py:39
  582.9 10.0 %fusion.358 = bf16[1,3,2048,256]{3,2,1,0:T(8,128)(2,1)S(1)} fusion(bf16[2048,1,3,256]{3,0,2,1:T(8,128)(2,1)S(1)} %copy-done, bf16[1,2048,2048]{2,1,0:T(8,128)(2,1)} %all-gather.19.cloned.1.call-done, f32[2048]{0:T(1024)S(1)} %copy-done.23, f32[2048]{0:T(1024)S(1)} %copy-done.18, f32[2048]{0:T(1024)S(1)} %copy-done.25, f32[2048]{0:T(1024)S(1)} %copy-done.26), kind=kOutput, calls=%fused_computation.423 | convolution fusion | flops 6469189632 | bytes 14712832 | tf_op jit(solution)/shard_map/sd,dgjh->gjsh/dot_general | solution.py:26
  592.9 2.4 fusion.51
  595.3 5.7 copy-done.10
  601.0 4.7 fusion.45
  605.7 43.3 %fusion.136 = f32[2048,2048]{1,0:T(8,128)} fusion(bf16[1024,2048]{1,0:T(8,128)(2,1)} %param.13, bf16[2048,1024]{1,0:T(8,128)(2,1)} %param.12, bf16[1,2048,2048]{2,1,0:T(8,128)(2,1)} %all-gather.19.cloned.1.call-done, f32[2048]{0:T(1024)S(1)} %copy-done.23, f32[2048]{0:T(1024)S(1)} %copy-done.18, f32[2048]{0:T(1024)S(1)} %copy-done.25, f32[2048]{0:T(1024)S(1)} %copy-done.26), kind=kOutput, calls=%fused_computation.225 | convolution fusion | flops 17341349888 | bytes 33587200 | tf_op jit(solution)/shard_map/sf,fd->sd/dot_general | solution.py:42
  649.0 17.7 %add_convert_fusion.2 = bf16[2048,2048]{1,0:T(8,128)(2,1)} fusion(f32[2048,2048]{1,0:T(8,128)} %fusion.136, bf16[256,2048]{1,0:T(8,128)(2,1)} %param.11, f32[2048,2048]{0,1:T(8,128)} %copy-done.10, f32[2048]{0:T(1024)S(1)} %fusion.45, f32[2048]{0:T(1024)S(1)} %get-tuple-element.17, bf16[1,3,2048,256]{3,2,1,0:T(8,128)(2,1)} %copy-done.30), kind=kOutput, calls=%fused_computation.62 | convolution fusion | flops 4329046016 | bytes 44056576 | tf_op jit(solution)/shard_map/gjsh,gjhd->sd/dot_general | solution.py:39
  667.4 10.0 %fusion.353 = bf16[1,3,2048,256]{3,2,1,0:T(8,128)(2,1)S(1)} fusion(bf16[2048,1,3,256]{3,0,2,1:T(8,128)(2,1)S(1)} %copy-done, bf16[1,2048,2048]{2,1,0:T(8,128)(2,1)} %all-gather.21.cloned.1.call-done, f32[2048]{0:T(1024)S(1)} %copy-done.21, f32[2048]{0:T(1024)S(1)} %copy-done.14, f32[2048]{0:T(1024)S(1)} %copy-done.25, f32[2048]{0:T(1024)S(1)} %copy-done.26), kind=kOutput, calls=%fused_computation.422 | convolution fusion | flops 6469189632 | bytes 14712832 | tf_op jit(solution)/shard_map/sd,dgjh->gjsh/dot_general | solution.py:26
  677.5 2.4 fusion.52
  679.9 5.7 copy-done.11
  685.6 4.7 fusion.46
  690.2 43.3 %fusion.134 = f32[2048,2048]{1,0:T(8,128)} fusion(bf16[1024,2048]{1,0:T(8,128)(2,1)} %param.13, bf16[2048,1024]{1,0:T(8,128)(2,1)} %param.12, bf16[1,2048,2048]{2,1,0:T(8,128)(2,1)} %all-gather.21.cloned.1.call-done, f32[2048]{0:T(1024)S(1)} %copy-done.21, f32[2048]{0:T(1024)S(1)} %copy-done.14, f32[2048]{0:T(1024)S(1)} %copy-done.25, f32[2048]{0:T(1024)S(1)} %copy-done.26), kind=kOutput, calls=%fused_computation.224 | convolution fusion | flops 17341349888 | bytes 33587200 | tf_op jit(solution)/shard_map/sf,fd->sd/dot_general | solution.py:42
  733.5 17.7 %add_convert_fusion.1 = bf16[2048,2048]{1,0:T(8,128)(2,1)} fusion(f32[2048,2048]{1,0:T(8,128)} %fusion.134, bf16[256,2048]{1,0:T(8,128)(2,1)} %param.11, f32[2048,2048]{0,1:T(8,128)} %copy-done.11, f32[2048]{0:T(1024)S(1)} %fusion.46, f32[2048]{0:T(1024)S(1)} %get-tuple-element.19, bf16[1,3,2048,256]{3,2,1,0:T(8,128)(2,1)} %copy-done.31), kind=kOutput, calls=%fused_computation.58 | convolution fusion | flops 4329046016 | bytes 44056576 | tf_op jit(solution)/shard_map/gjsh,gjhd->sd/dot_general | solution.py:39
  752.0 10.0 %fusion.348 = bf16[1,3,2048,256]{3,2,1,0:T(8,128)(2,1)S(1)} fusion(bf16[2048,1,3,256]{3,0,2,1:T(8,128)(2,1)S(1)} %copy-done, bf16[1,2048,2048]{2,1,0:T(8,128)(2,1)} %all-gather.23.cloned.1.call-done, f32[2048]{0:T(1024)S(1)} %copy-done.22, f32[2048]{0:T(1024)S(1)} %copy-done.16, f32[2048]{0:T(1024)S(1)} %copy-done.25, f32[2048]{0:T(1024)S(1)} %copy-done.26), kind=kOutput, calls=%fused_computation.421 | convolution fusion | flops 6469189632 | bytes 14712832 | tf_op jit(solution)/shard_map/sd,dgjh->gjsh/dot_general | solution.py:26
  762.0 2.4 fusion.53
  764.4 5.7 copy-done.12
  770.1 4.7 fusion.47
  774.8 43.2 %fusion.132 = f32[2048,2048]{1,0:T(8,128)} fusion(bf16[1024,2048]{1,0:T(8,128)(2,1)} %param.13, bf16[2048,1024]{1,0:T(8,128)(2,1)} %param.12, bf16[1,2048,2048]{2,1,0:T(8,128)(2,1)} %all-gather.23.cloned.1.call-done, f32[2048]{0:T(1024)S(1)} %copy-done.22, f32[2048]{0:T(1024)S(1)} %copy-done.16, f32[2048]{0:T(1024)S(1)} %copy-done.25, f32[2048]{0:T(1024)S(1)} %copy-done.26), kind=kOutput, calls=%fused_computation.223 | convolution fusion | flops 17341349888 | bytes 33587200 | tf_op jit(solution)/shard_map/sf,fd->sd/dot_general | solution.py:42
  818.0 17.7 %add_convert_fusion = bf16[2048,2048]{1,0:T(8,128)(2,1)} fusion(f32[2048,2048]{1,0:T(8,128)} %fusion.132, bf16[256,2048]{1,0:T(8,128)(2,1)} %param.11, f32[2048,2048]{0,1:T(8,128)} %copy-done.12, f32[2048]{0:T(1024)S(1)} %fusion.47, f32[2048]{0:T(1024)S(1)} %get-tuple-element.21, bf16[1,3,2048,256]{3,2,1,0:T(8,128)(2,1)} %copy-done.32), kind=kOutput, calls=%fused_computation.54 | convolution fusion | flops 4329046016 | bytes 44056576 | tf_op jit(solution)/shard_map/gjsh,gjhd->sd/dot_general | solution.py:39
  835.8 2.9 fusion.393
  838.7 2.9 fusion.395
  841.6 2.9 fusion.397
  844.5 2.9 fusion.399
  847.4 37.2 %reduce-scatter.17.cloned.1.call-done = bf16[256,2048]{1,0:T(8,128)(2,1)} async-done(((bf16[2048,2048]{1,0:T(8,128)(2,1)}), bf16[256,2048]{1,0:T(8,128)(2,1)}) %reduce-scatter.17.cloned.1.call-update) | async-done | bytes 1048592 | tf_op jit(solution)/shard_map/reduce_scatter | solution.py:44
  884.6 2.9 fusion.401
  (99 shorter events, 12.0 us)
Async XLA Ops:
  6.5 61.7 %copy-start = (bf16[2048,1,3,256]{3,0,2,1:T(8,128)(2,1)S(1)}, bf16[2048,1,3,256]{3,0,2,1:T(8,128)(2,1)}, u32[]{:S(2)}) copy-start(bf16[2048,1,3,256]{3,0,2,1:T(8,128)(2,1)} %param.10) | copy-start | bytes 9437188
  6.6 53.6 %all-gather.13.cloned.1.call-start = ((), (), s32[]{:S(2)}) async-start(), calls=%async_computation.12 | async-start | bytes 9437184 | tf_op jit(solution)/shard_map/all_gather | solution.py:23
  9.1 59.2 %copy-start.25 = (f32[2048]{0:T(1024)S(1)}, f32[2048]{0:T(1024)}, u32[]{:S(2)}) copy-start(f32[2048]{0:T(1024)} %param.9) | copy-start | bytes 24580
  9.1 59.2 %copy-start.26 = (f32[2048]{0:T(1024)S(1)}, f32[2048]{0:T(1024)}, u32[]{:S(2)}) copy-start(f32[2048]{0:T(1024)} %param.8) | copy-start | bytes 24580
  9.1 190.0 %reduce-scatter.7.cloned.1.call-start = ((), (), s32[]{:S(2)}) async-start(), calls=%async_computation.6 | async-start | bytes 9437184 | tf_op jit(solution)/shard_map/reduce_scatter | solution.py:44
  60.2 5.8 copy-start.6
  76.3 2.4 copy-start.27
  78.7 5.7 copy-start.7
  150.1 102.4 %all-gather.15.cloned.1.call-start = ((), (), s32[]{:S(2)}) async-start(), calls=%async_computation.13 | async-start | bytes 9437184 | tf_op jit(solution)/shard_map/all_gather | solution.py:23
  205.5 95.2 %all-gather.17.cloned.1.call-start = ((), (), s32[]{:S(2)}) async-start(), calls=%async_computation.14 | async-start | bytes 9437184 | tf_op jit(solution)/shard_map/all_gather | solution.py:23
  206.1 142.7 %all-gather.19.cloned.1.call-start = ((), (), s32[]{:S(2)}) async-start(), calls=%async_computation.15 | async-start | bytes 9437184 | tf_op jit(solution)/shard_map/all_gather | solution.py:23
  206.7 190.2 %all-gather.21.cloned.1.call-start = ((), (), s32[]{:S(2)}) async-start(), calls=%async_computation.16 | async-start | bytes 9437184 | tf_op jit(solution)/shard_map/all_gather | solution.py:23
  207.4 282.3 %all-gather.23.cloned.1.call-start = ((), (), s32[]{:S(2)}) async-start(), calls=%async_computation.17 | async-start | bytes 9437184 | tf_op jit(solution)/shard_map/all_gather | solution.py:23
  208.2 627.6 %reduce-scatter.9.cloned.1.call-start = ((), (), s32[]{:S(2)}) async-start(), calls=%async_computation.7 | async-start | bytes 9437184 | tf_op jit(solution)/shard_map/reduce_scatter | solution.py:44
  252.5 5.8 copy-start.5
  300.7 5.8 copy-start.4
  306.5 2.3 copy-start.19
  348.8 5.8 copy-start.3
  354.6 2.3 copy-start.17
  397.0 5.8 copy-start.2
  402.7 12.9 %copy-start.13 = (f32[2048]{0:T(1024)}, f32[2048]{0:T(1024)S(1)}, u32[]{:S(2)}) copy-start(f32[2048]{0:T(1024)S(1)} %broadcast_multiply_fusion.1) | copy-start | bytes 24580
  415.7 2.4 copy-start.28
  418.1 5.7 copy-start.8
  489.5 8.8 copy-start.20
  489.6 8.8 copy-start.24
  489.6 349.1 %reduce-scatter.11.cloned.1.call-start = ((), (), s32[]{:S(2)}) async-start(), calls=%async_computation.8 | async-start | bytes 9437184 | tf_op jit(solution)/shard_map/reduce_scatter | solution.py:44
  489.7 5.8 copy-start.1
  495.4 13.0 %copy-start.15 = (f32[2048]{0:T(1024)}, f32[2048]{0:T(1024)S(1)}, u32[]{:S(2)}) copy-start(f32[2048]{0:T(1024)S(1)} %broadcast_multiply_fusion) | copy-start | bytes 24580
  508.4 2.4 copy-start.29
  510.8 5.7 copy-start.9
  582.2 0.7 copy-start.18
  582.2 0.7 copy-start.23
  582.2 259.3 %reduce-scatter.13.cloned.1.call-start = ((), (), s32[]{:S(2)}) async-start(), calls=%async_computation.9 | async-start | bytes 9437184 | tf_op jit(solution)/shard_map/reduce_scatter | solution.py:44
  592.9 2.4 copy-start.30
  595.3 5.7 copy-start.10
  666.7 0.7 copy-start.14
  666.7 0.7 copy-start.21
  666.8 177.7 %reduce-scatter.15.cloned.1.call-start = ((), (), s32[]{:S(2)}) async-start(), calls=%async_computation.10 | async-start | bytes 9437184 | tf_op jit(solution)/shard_map/reduce_scatter | solution.py:44
  677.4 2.4 copy-start.31
  679.9 5.7 copy-start.11
  751.2 0.7 copy-start.16
  751.2 0.7 copy-start.22
  751.3 133.3 %reduce-scatter.17.cloned.1.call-start = ((), (), s32[]{:S(2)}) async-start(), calls=%async_computation.11 | async-start | bytes 9437184 | tf_op jit(solution)/shard_map/reduce_scatter | solution.py:44
  762.0 2.4 copy-start.32
  764.4 5.7 copy-start.12
Sparse Core Ops, SparseCore 0:
  9.2 50.9 all-gather.12
  150.3 48.7 reduce-scatter.6
  205.6 46.9 all-gather.14
  254.0 46.6 all-gather.16
  302.2 46.6 all-gather.18
  350.3 46.6 all-gather.20
  398.6 46.6 all-gather.22
  489.7 48.7 reduce-scatter.8
  582.4 48.7 reduce-scatter.10
  666.9 48.7 reduce-scatter.12
  751.4 48.7 reduce-scatter.14
  835.8 48.7 reduce-scatter.16

commit v2 on v1

v2 whole, which is shorter than its diff:
```python
import functools

import jax
import jax.numpy as jnp
from jax import lax
from jax.experimental import pallas as pl
from jax.experimental.pallas import tpu as pltpu
from jax.sharding import PartitionSpec as P

LN_EPS = 1e-5
MESH = pl.DeviceIdType.MESH
BF16 = jnp.bfloat16
F32 = jnp.float32
LOG2E = 1.4426950408889634
VMEM_LIMIT = 67_043_328


def layer_kernel(dims, x, gain, bias, w_qkv, w_out, w_up, w_dn,
                 y, xg, part, r1, fin, fin2,
                 wq, wu, wd, n, qkv, xt, ho, stage, r1v, addv, acc, m_s, l_s,
                 own_s, own_r, sib_s, sib_r, fwd_s, fwd_r, w_l, w_s, w_r,
                 h1_s, h1_r, h2n_s, h2n_r, h2d_s, h2d_r, sp_s, sp_r,
                 xt_sem, st_sem, ld_sem, fl_sem, fo_sem):
    chips, n_seq, rows, d_model, head, ff, chunk, ln_rows = dims
    ns = n_seq // 2
    half = rows // 2
    blk = 2 * rows
    scale = LOG2E * head ** -0.5

    me = lax.axis_index("tp")
    c, k = lax.div(me, 2), lax.rem(me, 2)
    o = 1 - k
    right, left, opp = lax.rem(c + 1, chips), lax.rem(c + chips - 1, chips), lax.rem(c + 2, chips)

    def dev(chip, core):
        return {"tp": 2 * chip + core}

    def row(chip, core, extra=0):
        return pl.multiple_of((2 * chip + core) * rows + extra, half)

    def remote(src, dst, send, recv, to):
        return pltpu.make_async_remote_copy(src_ref=src, dst_ref=dst, send_sem=send, recv_sem=recv,
                                            device_id=to, device_id_type=MESH)

    def own(s, kk, d):
        return remote(x.at[2 * s + kk], xg.at[s, pl.ds(row(c, k), rows)],
                      own_s.at[s, kk, d], own_r.at[s, k, d], dev(right if d == 0 else left, kk))

    def own_in(s, j, d):
        blk_ref = xg.at[s, pl.ds(row(left if d == 0 else right, j), rows)]
        return remote(blk_ref, blk_ref, own_s.at[s, j, d], own_r.at[s, j, d], dev(c, k))

    def sib(s):
        return remote(x.at[2 * s + o], xg.at[s, pl.ds(row(c, k), rows)], sib_s.at[s], sib_r.at[s], dev(c, o))

    def sib_in(s):
        ref = xg.at[s, pl.ds(row(c, o), rows)]
        return remote(ref, ref, sib_s.at[s], sib_r.at[s], dev(c, o))

    def fwd(s, j, d):
        at = row(left, j) if d == 0 else row(right, j, half)
        ref = xg.at[s, pl.ds(at, half)]
        return remote(ref, ref, fwd_s.at[s, j, d], fwd_r.at[s, j, d], dev(right if d == 0 else left, k))

    def fwd_in(s, j, d):
        ref = xg.at[s, pl.ds(row(opp, j, d * half), half)]
        return remote(ref, ref, fwd_s.at[s, j, d], fwd_r.at[s, j, d], dev(c, k))

    def hop1(s, j, d):
        return remote(part.at[s, pl.ds(row(opp, j, d * half), half)], r1.at[s, d, j],
                      h1_s.at[s, j, d], h1_r.at[s, j, d], dev(right if d == 0 else left, k))

    def hop1_in(s, j, d):
        return remote(r1.at[s, d, j], r1.at[s, d, j], h1_s.at[s, j, d], h1_r.at[s, j, d], dev(c, k))

    def hop2n(s, j, d):
        to = right if d == 0 else left
        off = (1 - d) * half
        return remote(part.at[s, pl.ds(row(to, j, off), half)], fin.at[2 * s + k, d, pl.ds(off, half)],
                      h2n_s.at[s, j, d], h2n_r.at[s, k, d], dev(to, j))

    def hop2n_in(s, kk, d):
        ref = fin.at[2 * s + kk, d, pl.ds((1 - d) * half, half)]
        return remote(ref, ref, h2n_s.at[s, 0, d], h2n_r.at[s, kk, d], dev(c, k))

    def hop2d(s, j, d):
        to = right if d == 0 else left
        return remote(addv.at[lax.rem(s, 2), d, j], fin.at[2 * s + k, d, pl.ds(d * half, half)],
                      h2d_s.at[s, j, d], h2d_r.at[s, k, d], dev(to, j))

    def hop2d_in(s, kk, d):
        ref = fin.at[2 * s + kk, d, pl.ds(d * half, half)]
        return remote(ref, ref, h2d_s.at[s, 0, d], h2d_r.at[s, kk, d], dev(c, k))

    def sibp(s):
        return remote(part.at[s, pl.ds(row(c, o), rows)], fin2.at[s], sp_s.at[s], sp_r.at[s], dev(c, o))

    def sibp_in(s):
        return remote(fin2.at[s], fin2.at[s], sp_s.at[s], sp_r.at[s], dev(c, o))

    both = [(j, d) for j in range(2) for d in range(2)]

    def weight_pairs():
        for t in range(3):
            yield w_qkv.at[t], wq.at[:, pl.ds(pl.multiple_of((2 * t + k) * head, head), head)], \
                wq.at[:, pl.ds(pl.multiple_of((2 * t + o) * head, head), head)]
        yield w_up, wu.at[:, pl.ds(pl.multiple_of(k * ff, ff), ff)], wu.at[:, pl.ds(pl.multiple_of(o * ff, ff), ff)]
        yield w_out, wd.at[pl.ds(pl.multiple_of(k * head, head), head)], \
            wd.at[pl.ds(pl.multiple_of(o * head, head), head)]
        yield w_dn, wd.at[pl.ds(pl.multiple_of(2 * head + k * ff, head), ff)], \
            wd.at[pl.ds(pl.multiple_of(2 * head + o * ff, head), ff)]

    def weights_local(i, src, mine):
        return pltpu.make_async_copy(src, mine, w_l.at[i])

    def wait_weights(lo, hi):
        for i, (src, mine, theirs) in enumerate(weight_pairs()):
            if lo <= i < hi:
                weights_local(i, src, mine).wait()
                remote(theirs, theirs, w_s.at[i], w_r.at[i], dev(c, o)).wait_recv()

    barrier = pltpu.get_barrier_semaphore()
    for to in (dev(c, o), dev(right, 0), dev(right, 1), dev(left, 0), dev(left, 1)):
        pl.semaphore_signal(barrier, inc=1, device_id=to, device_id_type=MESH)
    pl.semaphore_wait(barrier, 5)

    for kk in (k, o):
        for d in range(2):
            own(0, kk, d).start()
    sib(0).start()
    for i, (src, mine, theirs) in enumerate(weight_pairs()):
        weights_local(i, src, mine).start()
        remote(src, mine, w_s.at[i], w_r.at[i], dev(c, o)).start()
    for s in range(1, ns):
        sib(s).start()
    for j in (k, o):
        for d in range(2):
            own_in(0, j, d).wait_recv()
            fwd(0, j, d).start()
    for kk in (k, o):
        for d in range(2):
            own(1, kk, d).start()
    for d in range(2):
        own(2, k, d).start()

    def tile_start(s, slot, cb):
        for j in range(2):
            mine = (cb == c) & (k == j)
            dst = xt.at[slot, pl.ds(j * rows, rows)]

            @pl.when(mine)
            def _():
                pltpu.make_async_copy(x.at[2 * s + k], dst, xt_sem.at[slot, j]).start()

            @pl.when(jnp.logical_not(mine))
            def _():
                pltpu.make_async_copy(xg.at[s, pl.ds(row(cb, j), rows)], dst, xt_sem.at[slot, j]).start()

    def tile_wait(s, slot, cb):
        for j in range(2):
            pltpu.make_async_copy(xg.at[s, pl.ds(row(cb, j), rows)], xt.at[slot, pl.ds(j * rows, rows)],
                                  xt_sem.at[slot, j]).wait()

    def block_a(i):
        return lax.rem(c + jnp.where(i == 0, 0, jnp.where(i == 1, 3, jnp.where(i == 2, 1, 2))), chips)

    def block_b(i):
        return lax.rem(c + jnp.where(i == 0, 2, jnp.where(i == 1, 1, jnp.where(i == 2, 3, 0))), chips)

    def project(slot, cb):
        base = pl.multiple_of(cb * blk, blk)

        def norm(g, _):
            r0 = pl.multiple_of(g * ln_rows, ln_rows)
            v = xt[slot, pl.ds(r0, ln_rows), :].astype(F32)
            mean = jnp.mean(v, axis=-1, keepdims=True)
            cen = v - mean
            var = jnp.mean(cen * cen, axis=-1, keepdims=True)
            out = cen * lax.rsqrt(var + LN_EPS) * gain[...] + bias[...]
            n[pl.ds(pl.multiple_of(base + r0, ln_rows), ln_rows), :] = out.astype(BF16)
            return 0

        lax.fori_loop(0, blk // ln_rows, norm, 0)

        def proj(g, _):
            cols = pl.ds(pl.multiple_of(g * 2 * head, 2 * head), 2 * head)
            qkv[pl.ds(base, blk), cols] = jnp.dot(
                n[pl.ds(base, blk), :], wq[:, cols], preferred_element_type=F32).astype(BF16)
            return 0

        lax.fori_loop(0, 3, proj, 0)

    def dot_t(a, b):
        return lax.dot_general(a, b, (((1,), (1,)), ((), ())), preferred_element_type=F32)

    def attend(cb):
        base = pl.multiple_of(cb * blk, blk)
        mine = pl.ds(base, blk)
        causal = (lax.broadcasted_iota(jnp.int32, (blk, blk), 0)
                  >= lax.broadcasted_iota(jnp.int32, (blk, blk), 1))
        for h in range(2):
            q, key, val = (qkv[mine, pl.ds((2 * t + h) * head, head)] for t in range(3))
            sc = jnp.where(causal, dot_t(q, key), -jnp.inf)
            top = jnp.max(sc, axis=-1, keepdims=True)
            p = jnp.exp2((sc - top) * scale)
            m_s[h] = top
            l_s[h] = jnp.sum(p, axis=-1, keepdims=True)
            acc[h] = jnp.dot(p.astype(BF16), val, preferred_element_type=F32)

        def earlier(t, _):
            there = pl.ds(pl.multiple_of(t * blk, blk), blk)
            for h in range(2):
                q = qkv[mine, pl.ds(h * head, head)]
                key = qkv[there, pl.ds((2 + h) * head, head)]
                val = qkv[there, pl.ds((4 + h) * head, head)]
                sc = dot_t(q, key)
                old = m_s[h]
                top = jnp.maximum(old, jnp.max(sc, axis=-1, keepdims=True))
                p = jnp.exp2((sc - top) * scale)
                fade = jnp.exp2((old - top) * scale)
                m_s[h] = top
                l_s[h] = l_s[h] * fade + jnp.sum(p, axis=-1, keepdims=True)
                acc[h] = acc[h] * fade + jnp.dot(p.astype(BF16), val, preferred_element_type=F32)
            return 0

        lax.fori_loop(0, cb, earlier, 0)
        for h in range(2):
            ho[:, pl.ds(h * head, head)] = (acc[h] / l_s[h]).astype(BF16)

    def stage_copy(s, cb):
        return pltpu.make_async_copy(stage, part.at[s, pl.ds(pl.multiple_of(cb * blk, blk), blk)], st_sem)

    def mlp(s, i, cb):
        base = pl.multiple_of(cb * blk, blk)

        def up(g, _):
            hid = jnp.dot(n[pl.ds(base, blk), :], wu[:, pl.ds(pl.multiple_of(g * chunk, chunk), chunk)],
                          preferred_element_type=F32)
            act = 0.5 * hid * (1.0 + lax.erf(hid * 0.7071067811865476))
            ho[:, pl.ds(pl.multiple_of(2 * head + g * chunk, 2 * head), chunk)] = act.astype(BF16)
            return 0

        lax.fori_loop(0, 2 * ff // chunk, up, 0)

        @pl.when((s > 0) | (i > 0))
        def _():
            stage_copy(s, cb).wait()

        def down(g, _):
            cols = pl.ds(pl.multiple_of(g * chunk, chunk), chunk)
            stage[:, cols] = jnp.dot(ho[...], wd[:, cols], preferred_element_type=F32).astype(BF16)
            return 0

        lax.fori_loop(0, d_model // chunk, down, 0)
        stage_copy(s, cb).start()

    def add_and_send(s):
        slot = lax.rem(s, 2)

        @pl.when(s >= 2)
        def _():
            for j, d in both:
                hop2d(s - 2, j, d).wait_send()

        def loads(j, d):
            at = row(right, j) if d == 0 else row(left, j, half)
            return (pltpu.make_async_copy(part.at[s, pl.ds(at, half)], addv.at[slot, d, j], ld_sem.at[0, j, d]),
                    pltpu.make_async_copy(r1.at[s, d, j], r1v.at[d, j], ld_sem.at[1, j, d]))

        for j, d in both:
            hop1_in(s, j, d).wait_recv()
            for ld in loads(j, d):
                ld.start()
        for j, d in both:
            for ld in loads(j, d):
                ld.wait()

            def add(g, _):
                rr = pl.ds(pl.multiple_of(g * ln_rows, ln_rows), ln_rows)
                addv[slot, d, j, rr, :] = (addv[slot, d, j, rr, :].astype(F32)
                                           + r1v[d, j, rr, :].astype(F32)).astype(BF16)
                return 0

            lax.fori_loop(0, half // ln_rows, add, 0)
            hop2d(s, j, d).start()

    def final_loads(s, rel):
        kk = k if rel == 0 else o
        b0 = rel * 4 * rows
        srcs = (x.at[2 * s + kk],
                part.at[s, pl.ds(row(c, k), rows)] if rel == 0 else fin2.at[s],
                fin.at[2 * s + kk, 0], fin.at[2 * s + kk, 1])
        return [pltpu.make_async_copy(src, n.at[pl.ds(b0 + a * rows, rows)], fl_sem.at[rel, a])
                for a, src in enumerate(srcs)]

    def final_store(s, rel):
        return pltpu.make_async_copy(n.at[pl.ds(rel * 4 * rows, rows)], y.at[2 * s + (k if rel == 0 else o)],
                                     fo_sem.at[rel])

    def final(s):
        for rel in range(2):
            kk = k if rel == 0 else o
            for d in range(2):
                hop2n_in(s, kk, d).wait_recv()
                hop2d_in(s, kk, d).wait_recv()
            if rel == 1:
                sibp_in(s).wait_recv()

            @pl.when(s > 0)
            def _():
                final_store(s, rel).wait()

            for ld in final_loads(s, rel):
                ld.start()
        for rel in range(2):
            for ld in final_loads(s, rel):
                ld.wait()

            def total(g, _):
                def piece(a):
                    return n[pl.ds(pl.multiple_of(rel * 4 * rows + a * rows + g * ln_rows, ln_rows), ln_rows), :]

                branch = (piece(1).astype(F32) + piece(2).astype(F32) + piece(3).astype(F32)).astype(BF16)
                res = (piece(0).astype(F32) + branch.astype(F32)).astype(BF16)
                n[pl.ds(pl.multiple_of(rel * 4 * rows + g * ln_rows, ln_rows), ln_rows), :] = res
                return 0

            lax.fori_loop(0, rows // ln_rows, total, 0)
            final_store(s, rel).start()

    wait_weights(0, 3)

    def sequence(s, _):
        sib_in(s).wait_recv()
        tile_start(s, 0, block_a(0))

        def stage_a(i, _):
            slot = lax.rem(i, 2)
            cb = block_a(i)

            @pl.when(i == 3)
            def _():
                for j, d in both:
                    fwd_in(s, j, d).wait_recv()
                tile_start(s, slot, cb)

            tile_wait(s, slot, cb)

            @pl.when(i < 2)
            def _():
                tile_start(s, 1 - slot, block_a(i + 1))

            project(slot, cb)
            return 0

        lax.fori_loop(0, 4, stage_a, 0)

        @pl.when(s == 0)
        def _():
            wait_weights(3, 6)

        def stage_b(i, _):
            cb = block_b(i)
            attend(cb)
            mlp(s, i, cb)

            @pl.when((s == 0) & (i == 2))
            def _():
                for j, d in both:
                    own_in(1, j, d).wait_recv()
                    fwd(1, j, d).start()
                for d in range(2):
                    own(2, o, d).start()

            @pl.when((s < 2) & (i == 3))
            def _():
                for j, d in both:
                    hop1(s, j, d).start()

            @pl.when((s == 1) & (i == 1))
            def _():
                for j, d in both:
                    own_in(2, j, d).wait_recv()
                    fwd(2, j, d).start()
                for j, d in both:
                    hop2n(0, j, d).start()

            @pl.when((s == 1) & (i == 2))
            def _():
                add_and_send(0)

            @pl.when((s == 1) & (i == 3))
            def _():
                for j, d in both:
                    hop2n(1, j, d).start()

            @pl.when((s > 0) & (i == 1))
            def _():
                sibp(s - 1).start()

            @pl.when((s == 2) & (i == 1))
            def _():
                for j, d in both:
                    hop1(2, j, d).start()

            return 0

        lax.fori_loop(0, 4, stage_b, 0)
        return 0

    lax.fori_loop(0, ns, sequence, 0)

    last = ns - 1
    stage_copy(last, block_b(3)).wait()
    add_and_send(1)
    for j, d in both:
        hop2n(last, j, d).start()
    sibp(last).start()
    final(0)
    add_and_send(last)
    final(1)
    final(last)
    for rel in range(2):
        final_store(last, rel).wait()

    for s in range(ns):
        for j, d in both:
            own(s, j, d).wait_send()
            fwd(s, j, d).wait_send()
            hop1(s, j, d).wait_send()
            hop2n(s, j, d).wait_send()
            if s >= ns - 2:
                hop2d(s, j, d).wait_send()
        sib(s).wait_send()
        sibp(s).wait_send()
    for i, (src, mine, theirs) in enumerate(weight_pairs()):
        remote(src, mine, w_s.at[i], w_r.at[i], dev(c, o)).wait_send()


def solution(mesh):
    tp = mesh.shape["tp"]

    def local_layer(x_blk, ln_gain, ln_bias, w_qkv, w_out, w_up, w_down):
        n_seq, rows, d_model = x_blk.shape
        head = w_qkv.shape[3]
        ff = w_up.shape[1]
        chips, ns, seq, blk, half = tp // 2, n_seq // 2, rows * tp, 2 * rows, rows // 2
        chunk = min(512, d_model, ff)
        ln_rows = min(32, half)
        dims = (chips, n_seq, rows, d_model, head, ff, chunk, ln_rows)
        dma = pltpu.SemaphoreType.DMA
        anyspace = pl.BlockSpec(memory_space=pl.ANY)
        vmem = pl.BlockSpec(memory_space=pltpu.VMEM)

        def hbm(*shape):
            return jax.ShapeDtypeStruct(shape, BF16)

        outs = pl.pallas_call(
            functools.partial(layer_kernel, dims),
            name="layer",
            out_shape=(hbm(n_seq, rows, d_model), hbm(ns, seq, d_model), hbm(ns, seq, d_model),
                       hbm(ns, 2, 2, half, d_model), hbm(n_seq, 2, rows, d_model), hbm(ns, rows, d_model)),
            in_specs=[anyspace, vmem, vmem, anyspace, anyspace, anyspace, anyspace],
            out_specs=(anyspace,) * 6,
            scratch_shapes=[
                pltpu.VMEM((d_model, 6 * head), BF16),
                pltpu.VMEM((d_model, 2 * ff), BF16),
                pltpu.VMEM((2 * head + 2 * ff, d_model), BF16),
                pltpu.VMEM((seq, d_model), BF16),
                pltpu.VMEM((seq, 6 * head), BF16),
                pltpu.VMEM((2, blk, d_model), BF16),
                pltpu.VMEM((blk, 2 * head + 2 * ff), BF16),
                pltpu.VMEM((blk, d_model), BF16),
                pltpu.VMEM((2, 2, half, d_model), BF16),
                pltpu.VMEM((2, 2, 2, half, d_model), BF16),
                pltpu.VMEM((2, blk, head), F32),
                pltpu.VMEM((2, blk, 1), F32),
                pltpu.VMEM((2, blk, 1), F32),
                dma((ns, 2, 2)), dma((ns, 2, 2)), dma((ns,)), dma((ns,)), dma((ns, 2, 2)), dma((ns, 2, 2)),
                dma((6,)), dma((6,)), dma((6,)),
                dma((ns, 2, 2)), dma((ns, 2, 2)), dma((ns, 2, 2)), dma((ns, 2, 2)), dma((ns, 2, 2)),
                dma((ns, 2, 2)), dma((ns,)), dma((ns,)),
                dma((2, 2)), dma, dma((2, 2, 2)), dma((2, 4)), dma((2,)),
            ],
            compiler_params=pltpu.CompilerParams(
                collective_id=0, has_side_effects=True, vmem_limit_bytes=VMEM_LIMIT),
        )(x_blk, ln_gain.reshape(1, d_model), ln_bias.reshape(1, d_model),
          jnp.transpose(w_qkv[:, 0], (1, 0, 2)), w_out, w_up, w_down)
        return outs[0]

    return jax.shard_map(
        local_layer, mesh=mesh,
        in_specs=(P("dp", "tp", None), P(), P(), P(None, "tp", None, None),
                  P("tp", None), P(None, "tp"), P("tp", None)),
        out_specs=P("dp", "tp", None), check_vma=False)
```

time: 909 us -> 436 us (0.48); the launches traced: 895 us -> 435 us
  matrix products: 438 us -> 0 us
  Pallas kernels: 0 us -> 429 us
  waiting for transfers between devices: 303 us -> 0 us
  other arithmetic: 93.5 us -> 0 us
  local copies, waits for them, and re-layouts: 44.7 us -> 6.61 us
  between operations: 14.5 us -> 0.01 us
    dot_general x24 -> x0, matrix products: 438 us -> none  [the longest x6 260 us: one_sequence(): jnp.einsum('sf,fd->sd', activated, w_down, preferred_element_type=jnp.flo...]
    pallas_call x0 -> x1, Pallas kernels: none -> 429 us  [local_layer(): pl.pallas_call(functools.partial(layer_kernel, dims), name='layer', out_s...]
    all_gather x6 -> x0, waiting for transfers between devices: 214 us -> none  [one_sequence(): x_full = lax.all_gather(x_seq, 'tp', axis=0, tiled=True)]
    reduce_scatter x6 -> x0, waiting for transfers between devices: 86.1 us -> none  [one_sequence(): lax.psum_scatter(branch_part, 'tp', scatter_dimension=0, tiled=True)]
    reduce_sum x18 -> x0, other arithmetic: 70.2 us -> none  [the longest x6 28.3 us: layer_norm(): row_mean = jnp.mean(x_f32, axis=-1, keepdims=True)]
    unnamed x66 -> x1, local copies, waits for them, and re-layouts: 42.2 us -> 6.61 us
    unnamed x4 -> x0, other arithmetic: 11.6 us -> none
  transfers between devices with their start and end apart: 12 -> 0, of which waited for: 7 -> 0; matrix products, arithmetic and copies ran while one was open for 49% -> 0% of each run, Pallas kernels for 0% -> 0%
where the time goes in v2:
time: 436 us; the launch traced here: 435 us
  Pallas kernels  429 us (98%)
  local copies, waits for them, and re-layouts  6.61 us (2%)
    pallas_call x1, Pallas kernels, local_layer(): pl.pallas_call(functools.partial(layer_kernel, dims), name='layer', out_s...  429 us

profile of v2, /device:TPU:81, one launch (start us, length us, event | category | flops | bytes accessed | tf_op | source)
XLA Modules:
  0.0 435.3 jit_solution(11416682349443117342)
XLA Ops:
  0.0 428.7 %layer.1 = (bf16[6,256,2048]{2,1,0:T(8,128)(2,1)}, bf16[3,2048,2048]{2,1,0:T(8,128)(2,1)}, bf16[3,2048,2048]{2,1,0:T(8,128)(2,1)}, bf16[3,2,2,128,2048]{4,3,2,1,...) custom-call(bf16[6,256,2048]{2,1,0:T(8,128)(2,1)} %x.1, f32[1,2048]{1,0:T(1,128)} %bitcast.6, ...), custom_call_target="tpu_custom_call" | custom-call | tf_op jit(solution)/shard_map/layer/pallas_call | solution.py:458
  428.7 6.6 %copy.9 = bf16[6,256,2048]{2,1,0:T(8,128)(2,1)} copy(bf16[6,256,2048]{2,1,0:T(8,128)(2,1)} %get-tuple-element.6) | data formatting | bytes 12582912

commit v3 on v1

v3 whole, which is shorter than its diff:
```python
import functools

import jax
import jax.numpy as jnp
from jax import lax
from jax.experimental import pallas as pl
from jax.experimental.pallas import tpu as pltpu
from jax.sharding import PartitionSpec as P

LN_EPS = 1e-5
MESH = pl.DeviceIdType.MESH
BF16 = jnp.bfloat16
F32 = jnp.float32
LOG2E = 1.4426950408889634
VMEM_LIMIT = 67_043_328

PHASES = (("a", 0), ("a", 1), ("m", 0), ("m", 1), ("a", 2), ("m", 2))
QKV, UP0, UP1, DN0, DN1, OUT = range(6)


def layer_kernel(dims, x, gain, bias, w_qkv, w_out, w_up, w_dn,
                 y, xg, nbuf, obuf, sibin, mid, fin,
                 wq, wu, wd, nt, xt, qkv, ot, ho, stage, cin, tbuf, acc, m_s, l_s,
                 w_l, wx_s, wx_r, wf_s, wf_r, xm_s, xm_r, xp_s, xp_r, xf_s, xf_r, xd_s, xd_r,
                 sp_s, sp_r, t_s, t_r, p_s, p_r,
                 xt_sem, no_sem, oo_sem, nl_sem, ol_sem, cl_sem, yo_sem):
    span, rows, d_model, head, ff, chunk, ln_rows = dims
    half = rows // 2
    blk = 2 * rows
    scale = LOG2E * head ** -0.5

    g, me = lax.axis_index("dp"), lax.axis_index("tp")
    c, j = lax.div(me, 2), lax.rem(me, 2)
    o = 1 - j
    pair = lax.div(c, 2)
    mate = c + 1 - 2 * lax.rem(c, 2)
    part = 3 - c
    far = 3 - mate
    zb, yb = lax.rem(g, 2), lax.rem(lax.div(g, span), 2)
    gz, gy = g + 1 - 2 * zb, g + span * (1 - 2 * yb)

    def dev(chip, core, group=g):
        return {"dp": group, "tp": 2 * chip + core}

    sib, mt, pt, zd, yd = dev(c, o), dev(mate, j), dev(part, j), dev(c, j, gz), dev(c, j, gy)

    def remote(src, dst, send, recv, to):
        return pltpu.make_async_remote_copy(src_ref=src, dst_ref=dst, send_sem=send, recv_sem=recv,
                                            device_id=to, device_id_type=MESH)

    def row(chip, core, extra=0):
        return pl.multiple_of((2 * chip + core) * rows + extra, half)

    quarter = 2 * yb + zb
    q_z, q_y, q_zy = quarter + 1 - 2 * zb, quarter + 2 - 4 * yb, 3 - quarter

    def w_rows(piece):
        return {QKV: d_model, UP0: d_model // 2, UP1: d_model // 2, DN0: ff // 2, DN1: ff // 2, OUT: head}[piece] // 4

    def w_at(piece, q, side, hold):
        n = w_rows(piece)
        size = n if side is None else n // 2
        off = q * n + (0 if side is None else side * size)
        if piece in (UP1, DN1):
            off = off + 4 * n
        if hold and piece in (DN0, DN1):
            off = off + ff
        if hold and piece == OUT:
            off = off + 2 * ff + head
        at = pl.ds(pl.multiple_of(off, n // 2), size)
        if piece == QKV:
            return wq.at[:, at, pl.ds(head, head)] if hold else w_qkv.at[:, at, :]
        if piece in (UP0, UP1):
            return wu.at[at, pl.ds(ff, ff)] if hold else w_up.at[at, :]
        return wd.at[at, :] if hold else (w_out if piece == OUT else w_dn).at[at, :]

    def w_own(i):
        src, dst = ((w_qkv, wq.at[:, :, pl.ds(0, head)]), (w_up, wu.at[:, pl.ds(0, ff)]),
                    (w_dn, wd.at[pl.ds(0, ff), :]), (w_out, wd.at[pl.ds(2 * ff, head), :]))[i]
        return pltpu.make_async_copy(src, dst, w_l.at[i])

    def wx(k):
        return remote(w_at(k, quarter, None, False), w_at(k, quarter, None, True), wx_s.at[k], wx_r.at[k], pt)

    def wx_in(k):
        ref = w_at(k, quarter, None, True)
        return remote(ref, ref, wx_s.at[k], wx_r.at[k], pt)

    def wf(k, i):
        ref = (w_at(k, quarter, None, True) if i < 2 else w_at(k, q_y, 1, True) if i == 2 else w_at(k, q_z, 0, True))
        return remote(ref, ref, wf_s.at[k, i], wf_r.at[k, i], yd if i in (1, 3) else zd)

    def wf_in(k, i):
        ref = w_at(k, (q_z, q_y, q_zy, q_zy)[i], (None, None, 1, 0)[i], True)
        return remote(ref, ref, wf_s.at[k, i], wf_r.at[k, i], yd if i in (1, 3) else zd)

    def pass_quarter(k):
        wx_in(k).wait_recv()
        wf(k, 0).start()
        wf(k, 1).start()

    def pass_halves(k):
        wf_in(k, 0).wait_recv()
        wf_in(k, 1).wait_recv()
        wf(k, 2).start()
        wf(k, 3).start()

    def have(k):
        wf_in(k, 2).wait_recv()
        wf_in(k, 3).wait_recv()

    def own_seq(s):
        return 2 * s + pair

    def other_seq(s):
        return 2 * s + 1 - pair

    def xm(s):
        return remote(x.at[own_seq(s)], xg.at[s, pl.ds(row(c, j), rows)], xm_s.at[s], xm_r.at[s], mt)

    def xm_in(s):
        ref = xg.at[s, pl.ds(row(mate, j), rows)]
        return remote(ref, ref, xm_s.at[s], xm_r.at[s], mt)

    def xp(s, h):
        return remote(x.at[other_seq(s), pl.ds(h * half, half)], xg.at[s, pl.ds(row(c, j, h * half), half)],
                      xp_s.at[s, h], xp_r.at[s, h], pt)

    def xp_in(s, h):
        ref = xg.at[s, pl.ds(row(part, j, h * half), half)]
        return remote(ref, ref, xp_s.at[s, h], xp_r.at[s, h], pt)

    def xf(s, h):
        ref = xg.at[s, pl.ds(row(part, j, h * half), half)]
        return remote(ref, ref, xf_s.at[s, h], xf_r.at[s, h], mt)

    def xf_in(s, h):
        ref = xg.at[s, pl.ds(row(far, j, h * half), half)]
        return remote(ref, ref, xf_s.at[s, h], xf_r.at[s, h], mt)

    def xd(s, i, core=j):
        if i == 0:
            dst = xg.at[s, pl.ds(row(c, core), rows)]
            return remote(x.at[own_seq(s)], dst, xd_s.at[s, i], xd_r.at[s, i], sib)
        ref = (xg.at[s, pl.ds(row(mate, core), rows)] if i == 1 else
               xg.at[s, pl.ds(row(part if i < 4 else far, core, (i % 2) * half), half)])
        return remote(ref, ref, xd_s.at[s, i], xd_r.at[s, i], sib)

    def xd_in(s, i):
        return xd(s, i, o)

    def relay_mate(s):
        xm_in(s).wait_recv()
        xd(s, 1).start()

    def relay_part(s, h):
        xp_in(s, h).wait_recv()
        xf(s, h).start()
        xd(s, 2 + h).start()

    def relay_far(s):
        for h in range(2):
            xf_in(s, h).wait_recv()
            xd(s, 4 + h).start()

    barrier = pltpu.get_barrier_semaphore()
    for to in (sib, mt, pt, zd, yd):
        pl.semaphore_signal(barrier, inc=1, device_id=to, device_id_type=MESH)
    pl.semaphore_wait(barrier, 5)

    wx(QKV).start()
    xm(0).start()
    xp(0, 0).start()
    xp(0, 1).start()
    for i in range(4):
        w_own(i).start()
    xd(0, 0).start()
    wx(UP0).start()
    for s in (1, 2):
        xd(s, 0).start()
    for h in range(2):
        xp(1, h).start()
    for k in (UP1, DN0, DN1, OUT):
        wx(k).start()
    for h in range(2):
        xp(2, h).start()

    pass_quarter(QKV)
    relay_mate(0)
    relay_part(0, 0)
    pass_halves(QKV)
    relay_part(0, 1)
    xm(1).start()
    w_own(0).wait()
    have(QKV)

    events = {
        (0, "tile", 1): [lambda: pass_quarter(UP0)],
        (0, "tile", 3): [lambda: pass_halves(UP0)],
        (0, "att", 3): [lambda: relay_mate(1), lambda: relay_part(1, 0), lambda: relay_part(1, 1)],
        (1, "tile", 0): [lambda: pass_quarter(UP1)],
        (1, "tile", 2): [lambda: pass_quarter(DN0), lambda: pass_halves(UP1)],
        (1, "tile", 3): [lambda: xm(2).start(), lambda: pass_quarter(DN1)],
        (1, "att", 1): [lambda: pass_quarter(OUT), lambda: pass_halves(DN0)],
        (1, "att", 3): [lambda: pass_halves(DN1), lambda: pass_halves(OUT)],
        (2, "mlp", 0): [lambda: relay_mate(2), lambda: relay_part(2, 0), lambda: relay_part(2, 1)],
    }

    def at(step, phase, i):
        for (p, st, k), acts in events.items():
            if st == step:
                @pl.when((phase == p) & (i == k))
                def _(acts=acts):
                    for act in acts:
                        act()

    def tile_chip(i):
        return jnp.where(i == 0, c, jnp.where(i == 1, mate, jnp.where(i == 2, part, far)))

    def mlp_chip(i):
        return jnp.where(i == 0, far, jnp.where(i == 1, mate, jnp.where(i == 2, part, c)))

    def tile_half(slot, core):
        return xt.at[slot, pl.ds(pl.multiple_of(core * rows, rows), rows)]

    def tile_copy(s, slot, i, core):
        return pltpu.make_async_copy(xg.at[s, pl.ds(row(tile_chip(i), core), rows)], tile_half(slot, core),
                                     xt_sem.at[slot, 0 if core is j else 1])

    def tile_start(s, slot, i):
        for kind, needs in enumerate(((0,), (1,), (2, 3), (4, 5))):
            @pl.when(i == kind)
            def _(needs=needs):
                for n in needs:
                    xd_in(s, n).wait_recv()

        @pl.when(i == 0)
        def _():
            pltpu.make_async_copy(x.at[own_seq(s)], tile_half(slot, j), xt_sem.at[slot, 0]).start()

        @pl.when(i > 0)
        def _():
            tile_copy(s, slot, i, j).start()

        tile_copy(s, slot, i, o).start()

    def tile_wait(s, slot, i):
        tile_copy(s, slot, i, j).wait()
        tile_copy(s, slot, i, o).wait()

    def n_out(s, slot, cb):
        return pltpu.make_async_copy(nt.at[slot], nbuf.at[s, pl.ds(pl.multiple_of(cb * blk, blk), blk)],
                                     no_sem.at[slot])

    def o_out(s, slot, cb):
        return pltpu.make_async_copy(ot.at[slot], obuf.at[s, pl.ds(pl.multiple_of(cb * blk, blk), blk)],
                                     oo_sem.at[slot])

    def project(slot, cb):
        def norm(r, _):
            rr = pl.ds(pl.multiple_of(r * ln_rows, ln_rows), ln_rows)
            v = xt[slot, rr, :].astype(F32)
            mean = jnp.mean(v, axis=-1, keepdims=True)
            cen = v - mean
            var = jnp.mean(cen * cen, axis=-1, keepdims=True)
            nt[slot, rr, :] = (cen * lax.rsqrt(var + LN_EPS) * gain[...] + bias[...]).astype(BF16)
            return 0

        lax.fori_loop(0, blk // ln_rows, norm, 0)
        base = pl.ds(pl.multiple_of(cb * blk, blk), blk)

        def proj(t, _):
            qkv[base, pl.ds(pl.multiple_of(t * 2 * head, 2 * head), 2 * head)] = jnp.dot(
                nt[slot], wq[t], preferred_element_type=F32).astype(BF16)
            return 0

        lax.fori_loop(0, 3, proj, 0)

    def dot_t(a, b):
        return lax.dot_general(a, b, (((1,), (1,)), ((), ())), preferred_element_type=F32)

    def attend(slot, cb):
        mine = pl.ds(pl.multiple_of(cb * blk, blk), blk)
        causal = (lax.broadcasted_iota(jnp.int32, (blk, blk), 0)
                  >= lax.broadcasted_iota(jnp.int32, (blk, blk), 1))
        for h in range(2):
            q, key, val = (qkv[mine, pl.ds((2 * t + h) * head, head)] for t in range(3))
            sc = jnp.where(causal, dot_t(q, key), -jnp.inf)
            top = jnp.max(sc, axis=-1, keepdims=True)
            p = jnp.exp2((sc - top) * scale)
            m_s[h] = top
            l_s[h] = jnp.sum(p, axis=-1, keepdims=True)
            acc[h] = jnp.dot(p.astype(BF16), val, preferred_element_type=F32)

        def earlier(t, _):
            there = pl.ds(pl.multiple_of(t * blk, blk), blk)
            for h in range(2):
                q = qkv[mine, pl.ds(h * head, head)]
                key = qkv[there, pl.ds((2 + h) * head, head)]
                val = qkv[there, pl.ds((4 + h) * head, head)]
                sc = dot_t(q, key)
                old = m_s[h]
                top = jnp.maximum(old, jnp.max(sc, axis=-1, keepdims=True))
                p = jnp.exp2((sc - top) * scale)
                fade = jnp.exp2((old - top) * scale)
                m_s[h] = top
                l_s[h] = l_s[h] * fade + jnp.sum(p, axis=-1, keepdims=True)
                acc[h] = acc[h] * fade + jnp.dot(p.astype(BF16), val, preferred_element_type=F32)
            return 0

        lax.fori_loop(0, cb, earlier, 0)
        for h in range(2):
            ot[slot, :, pl.ds(h * head, head)] = (acc[h] / l_s[h]).astype(BF16)

    def sp(s, i):
        return remote(stage.at[pl.ds(pl.multiple_of(o * rows, rows), rows)], sibin.at[s, i],
                      sp_s.at[s, i], sp_r.at[s, i], sib)

    def sp_in(s, i):
        return remote(sibin.at[s, i], sibin.at[s, i], sp_s.at[s, i], sp_r.at[s, i], sib)

    def to_mate(s, i):
        return remote(tbuf.at[i], mid.at[s, i], t_s.at[s, i], t_r.at[s, i], mt)

    def from_mate(s, i):
        return remote(mid.at[s, i], mid.at[s, i], t_s.at[s, i], t_r.at[s, i], mt)

    def to_part(s):
        return remote(tbuf.at[2], fin.at[s], p_s.at[s], p_r.at[s], pt)

    def from_part(s):
        return remote(fin.at[s], fin.at[s], p_s.at[s], p_r.at[s], pt)

    def cin_load(src, slot):
        return pltpu.make_async_copy(src, cin.at[slot], cl_sem.at[slot])

    def y_store(q, slot):
        return pltpu.make_async_copy(cin.at[slot], y.at[q], yo_sem.at[slot - 2])

    def add_loads(s, kind):
        loads = [cin_load(sibin.at[s, kind], 0)]
        if kind >= 2:
            loads.append(cin_load(mid.at[s, kind - 2], 1))
        if kind == 3:
            loads.append(cin_load(x.at[own_seq(s)], 2))
        return loads

    def add_start(s, kind):
        sp_in(s, kind).wait_recv()
        if kind >= 2:
            from_mate(s, kind - 2).wait_recv()

        @pl.when(s > 0)
        def _():
            if kind < 2:
                to_mate(s - 1, kind).wait_send()
            elif kind == 2:
                to_part(s - 1).wait_send()
            else:
                y_store(own_seq(s), 2).wait()

        for ld in add_loads(s, kind):
            ld.start()

    def add_finish(s, kind):
        for ld in add_loads(s, kind):
            ld.wait()

        def add(r, _):
            rr = pl.ds(pl.multiple_of(r * ln_rows, ln_rows), ln_rows)
            mine = pl.ds(pl.multiple_of(j * rows + r * ln_rows, ln_rows), ln_rows)
            total = stage[mine, :].astype(F32) + cin[0, rr, :].astype(F32)
            if kind >= 2:
                total = total + cin[1, rr, :].astype(F32)
            total = total.astype(BF16)
            if kind == 3:
                cin[2, rr, :] = (cin[2, rr, :].astype(F32) + total.astype(F32)).astype(BF16)
            else:
                tbuf[kind, rr, :] = total
            return 0

        lax.fori_loop(0, rows // ln_rows, add, 0)
        sp(s, kind).wait_send()
        if kind < 2:
            to_mate(s, kind).start()
        elif kind == 2:
            to_part(s).start()
        else:
            y_store(own_seq(s), 2).start()

    def other_loads(s):
        return cin_load(fin.at[s], 0), cin_load(x.at[other_seq(s)], 3)

    def finish_other(s):
        from_part(s).wait_recv()

        @pl.when(s > 0)
        def _():
            y_store(other_seq(s), 3).wait()

        for ld in other_loads(s):
            ld.start()
        for ld in other_loads(s):
            ld.wait()

        def add(r, _):
            rr = pl.ds(pl.multiple_of(r * ln_rows, ln_rows), ln_rows)
            cin[3, rr, :] = (cin[3, rr, :].astype(F32) + cin[0, rr, :].astype(F32)).astype(BF16)
            return 0

        lax.fori_loop(0, rows // ln_rows, add, 0)
        y_store(other_seq(s), 3).start()

    def n_load(s, slot, i):
        return pltpu.make_async_copy(nbuf.at[s, pl.ds(pl.multiple_of(mlp_chip(i) * blk, blk), blk)], nt.at[slot],
                                     nl_sem.at[slot])

    def o_load(s, slot, i):
        return pltpu.make_async_copy(obuf.at[s, pl.ds(pl.multiple_of(mlp_chip(i) * blk, blk), blk)],
                                     ho.at[slot, :, pl.ds(2 * ff, 2 * head)], ol_sem.at[slot])

    def mlp_block(phase, s, i):
        slot = lax.rem(i, 2)
        chunks = 2 * ff // chunk
        n_load(s, slot, i).wait()

        def up(t, _):
            cols = pl.ds(pl.multiple_of(t * chunk, chunk), chunk)
            hid = jnp.dot(nt[slot], wu[:, cols], preferred_element_type=F32)
            ho[slot, :, cols] = (0.5 * hid * (1.0 + lax.erf(hid * 0.7071067811865476))).astype(BF16)
            return 0

        def pending(act):
            for kind in range(3):
                @pl.when(i == kind + 1)
                def _(kind=kind):
                    act(s, kind)

            @pl.when((i == 0) & (phase == 3))
            def _():
                act(s - 1, 3)

        def ups(u, _):
            lax.fori_loop(u * (chunks // 2), (u + 1) * (chunks // 2), up, 0)

            @pl.when(u == 0)
            def _():
                pending(add_start)

                @pl.when(i < 3)
                def _():
                    n_load(s, 1 - slot, i + 1).start()
                    o_load(s, 1 - slot, i + 1).start()

            return 0

        lax.fori_loop(0, 2, ups, 0)
        pending(add_finish)
        o_load(s, slot, i).wait()

        @pl.when((phase == 2) & (i == 0))
        def _():
            for k in (DN0, DN1, OUT):
                have(k)
            w_own(2).wait()
            w_own(3).wait()

        def down(t, _):
            cols = pl.ds(pl.multiple_of(t * chunk, chunk), chunk)
            stage[:, cols] = jnp.dot(ho[slot], wd[:, cols], preferred_element_type=F32).astype(BF16)
            return 0

        lax.fori_loop(0, d_model // chunk, down, 0)
        for kind in range(4):
            @pl.when(i == kind)
            def _(kind=kind):
                sp(s, kind).start()

    def pick(values, phase):
        out = jnp.int32(values[0])
        for p in range(1, len(values)):
            out = jnp.where(phase == p, values[p], out)
        return out

    def run(phase, _):
        s = pick([s for _, s in PHASES], phase)
        is_a = pick([int(kind == "a") for kind, _ in PHASES], phase) == 1

        @pl.when(is_a)
        def _():
            tile_start(s, 0, 0)

            def tile(i, _):
                slot = lax.rem(i, 2)
                cb = tile_chip(i)

                @pl.when(i == 3)
                def _():
                    relay_far(s)
                    tile_start(s, slot, i)

                tile_wait(s, slot, i)

                @pl.when(i < 2)
                def _():
                    tile_start(s, 1 - slot, i + 1)

                @pl.when(i >= 2)
                def _():
                    n_out(s, slot, cb).wait()

                project(slot, cb)
                n_out(s, slot, cb).start()

                @pl.when((phase == 4) & (i == 0))
                def _():
                    add_start(s - 1, 3)
                    add_finish(s - 1, 3)

                at("tile", phase, i)
                return 0

            lax.fori_loop(0, 4, tile, 0)

            def att(i, _):
                slot = lax.rem(i, 2)

                @pl.when(i >= 2)
                def _():
                    o_out(s, slot, i).wait()

                attend(slot, i)
                o_out(s, slot, i).start()
                at("att", phase, i)
                return 0

            lax.fori_loop(0, 4, att, 0)
            for slot in range(2):
                n_out(s, slot, 0).wait()
                o_out(s, slot, 0).wait()

        @pl.when(jnp.logical_not(is_a))
        def _():
            n_load(s, 0, 0).start()
            o_load(s, 0, 0).start()

            @pl.when(phase == 2)
            def _():
                for k in (UP0, UP1):
                    have(k)
                w_own(1).wait()

            def block(i, _):
                mlp_block(phase, s, i)
                at("mlp", phase, i)

                @pl.when((s > 0) & (i == 2))
                def _():
                    finish_other(s - 1)

                return 0

            lax.fori_loop(0, 4, block, 0)

        return 0

    lax.fori_loop(0, len(PHASES), run, 0)

    add_start(jnp.int32(2), 3)
    add_finish(jnp.int32(2), 3)
    finish_other(jnp.int32(2))

    for s in range(3):
        xm(s).wait_send()
        for h in range(2):
            xp(s, h).wait_send()
            xf(s, h).wait_send()
        for i in range(6):
            xd(s, i).wait_send()
    for k in range(6):
        wx(k).wait_send()
        for i in range(4):
            wf(k, i).wait_send()
    to_mate(2, 0).wait_send()
    to_mate(2, 1).wait_send()
    to_part(2).wait_send()
    y_store(own_seq(2), 2).wait()
    y_store(other_seq(2), 3).wait()


def neighbour_span(groups):
    short = 1
    while short * short * 4 <= groups:
        short *= 2
    return groups // short


def solution(mesh):
    tp, groups = mesh.shape["tp"], mesh.shape["dp"]
    span = neighbour_span(groups)
    assert tp == 8 and groups % (2 * span) == 0 and span % 2 == 0

    def local_layer(x_blk, ln_gain, ln_bias, w_qkv, w_out, w_up, w_down):
        n_seq, rows, d_model = x_blk.shape
        head = w_qkv.shape[3]
        ff = w_up.shape[1]
        ns, seq, blk = n_seq // 2, rows * tp, 2 * rows
        assert ns == 3 and w_qkv.shape[1:3] == (1, 3)
        chunk = min(512, d_model, ff)
        ln_rows = min(32, rows // 2)
        dims = (span, rows, d_model, head, ff, chunk, ln_rows)
        dma = pltpu.SemaphoreType.DMA
        anyspace = pl.BlockSpec(memory_space=pl.ANY)
        vmem = pl.BlockSpec(memory_space=pltpu.VMEM)

        def hbm(*shape):
            return jax.ShapeDtypeStruct(shape, BF16)

        outs = pl.pallas_call(
            functools.partial(layer_kernel, dims),
            name="layer",
            out_shape=(hbm(n_seq, rows, d_model), hbm(ns, seq, d_model), hbm(ns, seq, d_model), hbm(ns, seq, 2 * head),
                       hbm(ns, 4, rows, d_model), hbm(ns, 2, rows, d_model), hbm(ns, rows, d_model)),
            in_specs=[anyspace, vmem, vmem, anyspace, anyspace, anyspace, anyspace],
            out_specs=(anyspace,) * 7,
            scratch_shapes=[
                pltpu.VMEM((3, d_model, 2 * head), BF16),
                pltpu.VMEM((d_model, 2 * ff), BF16),
                pltpu.VMEM((2 * ff + 2 * head, d_model), BF16),
                pltpu.VMEM((2, blk, d_model), BF16),
                pltpu.VMEM((2, blk, d_model), BF16),
                pltpu.VMEM((seq, 6 * head), BF16),
                pltpu.VMEM((2, blk, 2 * head), BF16),
                pltpu.VMEM((2, blk, 2 * ff + 2 * head), BF16),
                pltpu.VMEM((blk, d_model), BF16),
                pltpu.VMEM((4, rows, d_model), BF16),
                pltpu.VMEM((3, rows, d_model), BF16),
                pltpu.VMEM((2, blk, head), F32),
                pltpu.VMEM((2, blk, 1), F32),
                pltpu.VMEM((2, blk, 1), F32),
                dma((4,)), dma((6,)), dma((6,)), dma((6, 4)), dma((6, 4)),
                dma((ns,)), dma((ns,)), dma((ns, 2)), dma((ns, 2)), dma((ns, 2)), dma((ns, 2)),
                dma((ns, 6)), dma((ns, 6)),
                dma((ns, 4)), dma((ns, 4)), dma((ns, 2)), dma((ns, 2)), dma((ns,)), dma((ns,)),
                dma((2, 2)), dma((2,)), dma((2,)), dma((2,)), dma((2,)), dma((4,)), dma((2,)),
            ],
            compiler_params=pltpu.CompilerParams(
                collective_id=0, has_side_effects=True, vmem_limit_bytes=VMEM_LIMIT),
        )(x_blk, ln_gain.reshape(1, d_model), ln_bias.reshape(1, d_model),
          jnp.transpose(w_qkv[:, 0], (1, 0, 2)), w_out, w_up, w_down)
        return outs[0]

    return jax.shard_map(
        local_layer, mesh=mesh,
        in_specs=(P("dp", "tp", None), P(), P(), P(None, "tp", None, None),
                  P("tp", None), P(None, "tp"), P("tp", None)),
        out_specs=P("dp", "tp", None), check_vma=False)
```

time: 909 us -> 447 us (0.49); the launches traced: 895 us -> 447 us
  Pallas kernels: 0 us -> 440 us
  matrix products: 438 us -> 0 us
  waiting for transfers between devices: 303 us -> 0 us
  other arithmetic: 93.5 us -> 0 us
  local copies, waits for them, and re-layouts: 44.7 us -> 6.61 us
  between operations: 14.5 us -> 0.01 us
    pallas_call x0 -> x1, Pallas kernels: none -> 440 us  [local_layer(): pl.pallas_call(functools.partial(layer_kernel, dims), name='layer', out_s...]
    dot_general x24 -> x0, matrix products: 438 us -> none  [the longest x6 260 us: one_sequence(): jnp.einsum('sf,fd->sd', activated, w_down, preferred_element_type=jnp.flo...]
    all_gather x6 -> x0, waiting for transfers between devices: 214 us -> none  [one_sequence(): x_full = lax.all_gather(x_seq, 'tp', axis=0, tiled=True)]
    reduce_scatter x6 -> x0, waiting for transfers between devices: 86.1 us -> none  [one_sequence(): lax.psum_scatter(branch_part, 'tp', scatter_dimension=0, tiled=True)]
    reduce_sum x18 -> x0, other arithmetic: 70.2 us -> none  [the longest x6 28.3 us: layer_norm(): row_mean = jnp.mean(x_f32, axis=-1, keepdims=True)]
    unnamed x66 -> x1, local copies, waits for them, and re-layouts: 42.2 us -> 6.61 us
    unnamed x4 -> x0, other arithmetic: 11.6 us -> none
  transfers between devices with their start and end apart: 12 -> 0, of which waited for: 7 -> 0; matrix products, arithmetic and copies ran while one was open for 49% -> 0% of each run, Pallas kernels for 0% -> 0%
where the time goes in v3:
time: 447 us
  Pallas kernels  440 us (98%)
  local copies, waits for them, and re-layouts  6.61 us (1%)
    pallas_call x1, Pallas kernels, local_layer(): pl.pallas_call(functools.partial(layer_kernel, dims), name='layer', out_s...  440 us

profile of v3, /device:TPU:81, one launch (start us, length us, event | category | flops | bytes accessed | tf_op | source)
XLA Modules:
  0.0 446.6 jit_solution(1433322570117662473)
XLA Ops:
  0.0 439.9 %layer.1 = (bf16[6,256,2048]{2,1,0:T(8,128)(2,1)}, bf16[3,2048,2048]{2,1,0:T(8,128)(2,1)}, bf16[3,2048,2048]{2,1,0:T(8,128)(2,1)}, bf16[3,2048,512]{2,1,0:T(8,12...) custom-call(bf16[6,256,2048]{2,1,0:T(8,128)(2,1)} %x.1, ...), custom_call_target="tpu_custom_call" | custom-call | tf_op jit(solution)/shard_map/layer/pallas_call | solution.py:619
  439.9 6.6 %copy.9 = bf16[6,256,2048]{2,1,0:T(8,128)(2,1)} copy(bf16[6,256,2048]{2,1,0:T(8,128)(2,1)} %get-tuple-element.6) | data formatting | bytes 12582912

commit v4 on v3

--- a/solution.py
+++ b/solution.py
@@ -163,6 +163,12 @@
             xf_in(s, h).wait_recv()
             xd(s, 4 + h).start()
 
+    def send_x(s):
+        xm(s).start()
+        xd(s, 0).start()
+        for h in range(2):
+            xp(s, h).start()
+
     barrier = pltpu.get_barrier_semaphore()
     for to in (sib, mt, pt, zd, yd):
         pl.semaphore_signal(barrier, inc=1, device_id=to, device_id_type=MESH)
@@ -170,37 +176,31 @@
 
     wx(QKV).start()
     xm(0).start()
-    xp(0, 0).start()
-    xp(0, 1).start()
     for i in range(4):
         w_own(i).start()
     xd(0, 0).start()
-    wx(UP0).start()
-    for s in (1, 2):
-        xd(s, 0).start()
-    for h in range(2):
-        xp(1, h).start()
-    for k in (UP1, DN0, DN1, OUT):
-        wx(k).start()
-    for h in range(2):
-        xp(2, h).start()
+    xp(0, 0).start()
+    xp(0, 1).start()
 
     pass_quarter(QKV)
     relay_mate(0)
     relay_part(0, 0)
+    wx(UP0).start()
     pass_halves(QKV)
     relay_part(0, 1)
-    xm(1).start()
+    send_x(1)
     w_own(0).wait()
     have(QKV)
 
     events = {
         (0, "tile", 1): [lambda: pass_quarter(UP0)],
-        (0, "tile", 3): [lambda: pass_halves(UP0)],
-        (0, "att", 3): [lambda: relay_mate(1), lambda: relay_part(1, 0), lambda: relay_part(1, 1)],
-        (1, "tile", 0): [lambda: pass_quarter(UP1)],
+        (0, "tile", 3): [lambda: wx(UP1).start(), lambda: pass_halves(UP0)],
+        (0, "att", 1): [lambda: wx(DN0).start()],
+        (0, "att", 3): [lambda: relay_mate(1), lambda: relay_part(1, 0), lambda: relay_part(1, 1),
+                        lambda: wx(DN1).start()],
+        (1, "tile", 0): [lambda: pass_quarter(UP1), lambda: wx(OUT).start()],
         (1, "tile", 2): [lambda: pass_quarter(DN0), lambda: pass_halves(UP1)],
-        (1, "tile", 3): [lambda: xm(2).start(), lambda: pass_quarter(DN1)],
+        (1, "tile", 3): [lambda: send_x(2), lambda: pass_quarter(DN1)],
         (1, "att", 1): [lambda: pass_quarter(OUT), lambda: pass_halves(DN0)],
         (1, "att", 3): [lambda: pass_halves(DN1), lambda: pass_halves(OUT)],
         (2, "mlp", 0): [lambda: relay_mate(2), lambda: relay_part(2, 0), lambda: relay_part(2, 1)],

time: 447 us -> 447 us (level)
  no operation moved by 1% of the time
where the time goes in v4:
time: 447 us
  Pallas kernels  440 us (98%)
  local copies, waits for them, and re-layouts  6.61 us (1%)
    pallas_call x1, Pallas kernels, local_layer(): pl.pallas_call(functools.partial(layer_kernel, dims), name='layer', out_s...  440 us

profile of v4, /device:TPU:81, one launch (start us, length us, event | category | flops | bytes accessed | tf_op | source)
XLA Modules:
  0.0 446.7 jit_solution(8837616107567303229)
XLA Ops:
  0.0 440.0 %layer.1 = (bf16[6,256,2048]{2,1,0:T(8,128)(2,1)}, bf16[3,2048,2048]{2,1,0:T(8,128)(2,1)}, bf16[3,2048,2048]{2,1,0:T(8,128)(2,1)}, bf16[3,2048,512]{2,1,0:T(8,12...) custom-call(bf16[6,256,2048]{2,1,0:T(8,128)(2,1)} %x.1, ...), custom_call_target="tpu_custom_call" | custom-call | tf_op jit(solution)/shard_map/layer/pallas_call | solution.py:619
  440.1 6.6 %copy.9 = bf16[6,256,2048]{2,1,0:T(8,128)(2,1)} copy(bf16[6,256,2048]{2,1,0:T(8,128)(2,1)} %get-tuple-element.6) | data formatting | bytes 12582912
